TPU v7x, 16 devices: a 4x2x1 block of a 4x4x8 slice. The times are simulated.
16 devices in a mesh: dp: 2 (over y, z), tp: 8 (over x, core).
Axes of the slice: x: 4, y: 2, z: 1, core: 2. Of those that a mesh axis runs over, the one named last changes fastest.
The devices are a block of a 4x4x8 slice.
Arguments:
- x_norm: bfloat16 [8192, 1536], P(('dp', 'tp')), parts along dimension 0
- grad_y: bfloat16 [8192, 1536], P(('dp', 'tp')), parts along dimension 0
- u_gate: bfloat16 [8192, 8960], P('dp', 'tp'), parts along dimension 0
- u_up: bfloat16 [8192, 8960], P('dp', 'tp'), parts along dimension 0
- w_gate: bfloat16 [1536, 8960], P(None, 'tp')
- w_up: bfloat16 [1536, 8960], P(None, 'tp')
- w_down: bfloat16 [8960, 1536], P('tp')
- x_in: bfloat16 [8192, 1536], P(('dp', 'tp')), parts along dimension 0
- gamma: bfloat16 [1536], replicated
- grad_res: bfloat16 [8192, 1536], P(('dp', 'tp')), parts along dimension 0
- attn_out: bfloat16 [8192, 1536], P('dp', 'tp'), parts along dimension 0
- w_out: bfloat16 [1536, 1536], P('tp')
Outputs:
- output 1: bfloat16 [8192, 1536], P(('dp', 'tp')), parts along dimension 0
- output 2: bfloat16 [8192, 1536], P('dp', 'tp'), parts along dimension 0
- output 3: float32 [3072, 8960], P('dp', 'tp'), parts along dimension 0
- output 4: float32 [3072, 8960], P('dp', 'tp'), parts along dimension 0
- output 5: float32 [17920, 1536], P(('dp', 'tp')), parts along dimension 0
- output 6: float32 [3072, 1536], P(('dp', 'tp')), parts along dimension 0
There are 2 independent parts. A program takes and returns all parts, laid end to end along the dimension named above; an argument that names none is the same for every part.
All inputs are finite; a program needn't handle non-finite values.
Results may differ from a plain program's by a relative error of at most 0.014854.
Values are sent between devices in bfloat16 or wider.
A program may use at most 768 MiB of HBM per device.

v0:
```python
import functools

import jax
import jax.numpy as jnp
from jax import lax
from jax.experimental import pallas as pl
from jax.experimental.pallas import tpu as pltpu
from jax.sharding import PartitionSpec as P


NORM_EPS = 1e-5
CONTRACT_ROWS = (((0,), (0,)), ((), ()))
CONTRACT_COLS = (((1,), (1,)), ((), ()))
F32, BF16 = jnp.float32, jnp.bfloat16
MESH = pl.DeviceIdType.MESH
OWN, RIGHT, LEFT, FAR = range(4)


def dot_rows(a, b):
    return lax.dot_general(a, b, CONTRACT_ROWS, preferred_element_type=F32)


def dot_cols(a, b):
    return lax.dot_general(a, b, CONTRACT_COLS, preferred_element_type=F32)


def chip_step(slot):
    return lax.rem(slot * (slot + 1) // 2, 4)


def main_kernel(n, x_hbm, gy_hbm, ug_hbm, uu_hbm, wg_hbm, wu_hbm, wd_hbm, xin_hbm, gamma_ref, gres_hbm,
                x_all, dug_all, duu_all, gwg_hbm, gwu_hbm, gwd_hbm, ds_top, ds_low, other_top, other_low, left_top, right_low,
                wg, wu, wd, buf, ug, uu, z, dug, duu, acc, prec, hop, fin,
                w_sem, u_sem, o_sem, b_sem, ys, yd, yr, xs, xd, xr, ps, pr, hs, hr, fs, fr, qs, qr, ss, sr, ds_sem,
                as_, ar):
    me = lax.axis_index("tp")
    core, chip, chips = lax.rem(me, 2), me // 2, n // 2
    right = lax.rem(chip + 1, chips) * 2 + core
    left = lax.rem(chip + chips - 1, chips) * 2 + core
    other = chip * 2 + 1 - core
    rows = gy_hbm.shape[0]
    half = rows // 2
    quarter = half // 4
    ffn = wd.shape[0]
    gy = buf
    part = 8

    def half_of(h):
        return pl.ds(h * half, half)

    def x_at(slot, h):
        return x_all.at[pl.ds(slot * rows + h * half, half)]

    def remote(src, dst, send, recv, to):
        return pltpu.make_async_remote_copy(src_ref=src, dst_ref=dst, send_sem=send, recv_sem=recv,
                                            device_id={"tp": to}, device_id_type=MESH)

    def load_u(s, b):
        block = lax.rem(chip + chip_step(s // 2), chips) * 2 + lax.rem(core + lax.rem(s, 2), 2)
        cols = pl.ds(pl.multiple_of(block * rows, rows), rows)
        return (pltpu.make_async_copy(ug_hbm.at[:, cols], ug.at[b], u_sem.at[b, 0]),
                pltpu.make_async_copy(uu_hbm.at[:, cols], uu.at[b], u_sem.at[b, 1]))

    def store_u(s, b):
        cols = pl.ds(pl.multiple_of(s * rows, rows), rows)
        return (pltpu.make_async_copy(dug.at[b], dug_all.at[:, cols], o_sem.at[b, 0]),
                pltpu.make_async_copy(duu.at[b], duu_all.at[:, cols], o_sem.at[b, 1]))

    def y_first(d, h):
        land = 2 * (LEFT, RIGHT)[d]
        return remote(gy_hbm.at[half_of(h)], gy.at[land, half_of(h)], ys.at[d, h], yr.at[land, h], (right, left)[d])

    def y_second(d):
        src, h = 2 * (LEFT, RIGHT)[d], d
        return remote(gy.at[src, half_of(h)], gy.at[2 * FAR, half_of(h)], ys.at[d, 2], yr.at[2 * FAR, h],
                      (right, left)[d])

    def y_swap(slot, h):
        src = gy_hbm.at[half_of(h)] if slot == OWN else gy.at[2 * slot, half_of(h)]
        return remote(src, gy.at[2 * slot + 1, half_of(h)], yd.at[slot, h], yr.at[2 * slot + 1, h], other)

    def y_own(h):
        return pltpu.make_async_copy(gy_hbm.at[half_of(h)], gy.at[0, half_of(h)], yr.at[0, h])

    def x_first(d, h):
        land = 2 * (LEFT, RIGHT)[d]
        return remote(x_hbm.at[half_of(h)], x_at(land, h), xs.at[d, h], xr.at[land, h],
                      (right, left)[d])

    def x_second(d):
        src, h = 2 * (LEFT, RIGHT)[d], d
        return remote(x_at(src, h), x_at(2 * FAR, h), xs.at[d, 2], xr.at[2 * FAR, h], (right, left)[d])

    def x_swap(slot, h):
        src = x_hbm.at[half_of(h)] if slot == OWN else x_at(2 * slot, h)
        return remote(src, x_at(2 * slot + 1, h), xd.at[slot, h], xr.at[2 * slot + 1, h], other)

    x_in_copy = pltpu.make_async_copy(x_hbm, buf.at[part + FAR], b_sem.at[0])
    x_out_copy = pltpu.make_async_copy(buf.at[part + FAR], x_all.at[pl.ds(0, rows)], b_sem.at[1])

    def p_swap(slot):
        return remote(buf.at[2 * slot + 1], prec.at[slot], ps.at[slot], pr.at[slot], other)

    def r_first(d):
        return remote(buf.at[part + FAR, half_of(d)], hop.at[d], hs.at[d], hr.at[d], (right, left)[d])

    def r_last(d, h):
        src = part + (RIGHT, LEFT)[d]
        return remote(buf.at[src, half_of(h)], fin.at[d, half_of(h)], fs.at[d, h], fr.at[d, h], (right, left)[d])

    def r_final(d, q):
        rws = pl.ds(d * half + q * quarter, quarter)
        return remote(buf.at[part + (RIGHT, LEFT)[d], rws], fin.at[d, rws], qs.at[d, q], qr.at[d, q],
                      (right, left)[d])

    def s_swap(h, q):
        return remote(buf.at[2, pl.ds(h * half + q * quarter, quarter)],
                      (other_top, other_low)[h].at[pl.ds(q * quarter, quarter)], ss.at[h, q], sr.at[h, q], other)

    def s_first(d, q):
        return remote(buf.at[2, pl.ds(d * half + q * quarter, quarter)],
                      (left_top, right_low)[d].at[pl.ds(q * quarter, quarter)], as_.at[d, q], ar.at[d, q],
                      (right, left)[d])

    def s_out(h, q):
        return pltpu.make_async_copy(buf.at[2, pl.ds(h * half + q * quarter, quarter)],
                                     (ds_top, ds_low)[h].at[pl.ds(q * quarter, quarter)], ds_sem.at[h, q])

    weights = [pltpu.make_async_copy(a, b, w_sem.at[i])
               for i, (a, b) in enumerate(((wd_hbm, wd), (wg_hbm, wg), (wu_hbm, wu)))]
    gw_copies = [pltpu.make_async_copy(acc, a, w_sem.at[i]) for i, a in enumerate((gwd_hbm, gwg_hbm, gwu_hbm))]

    barrier = pltpu.get_barrier_semaphore()
    for peer in (right, left, other):
        pl.semaphore_signal(barrier, inc=1, device_id={"tp": peer}, device_id_type=MESH)
    for h in (0, 1):
        y_own(h).start()
    weights[0].start()
    for c in load_u(0, 0):
        c.start()
    weights[1].start()
    weights[2].start()
    x_in_copy.start()
    pl.semaphore_wait(barrier, 3)
    for step in (0, 1):
        y_first(0, step).start()
        y_first(1, 1 - step).start()
    for h in (0, 1):
        y_swap(OWN, h).start()

    fstep = ffn // 5

    def clear():
        def body(i, carry):
            acc[pl.ds(pl.multiple_of(i * 16, 16), 16), :] = jnp.zeros((16, acc.shape[1]), F32)
            return carry

        lax.fori_loop(0, ffn // 16, body, 0)

    def accumulate(a, b):
        for f in range(5):
            lines = pl.ds(f * fstep, fstep)
            acc[lines, :] += jnp.dot(a[lines, :], b[...], preferred_element_type=F32)

    clear()
    for c in weights:
        c.wait()

    def unit(s, carry):
        slot, plane, b = s // 2, lax.rem(s, 2), lax.rem(s, 2)

        @pl.when(s + 1 < 8)
        def _():
            for c in load_u(s + 1, lax.rem(s + 1, 2)):
                c.start()

        @pl.when(s == 2)
        def _():
            y_first(0, 0).wait_recv()
            y_second(0).start()
            y_first(1, 1).wait_recv()
            y_second(1).start()
            y_swap(LEFT, 0).start()
            y_swap(RIGHT, 1).start()
            for step in (0, 1):
                x_first(0, step).start()
                x_first(1, 1 - step).start()
            x_in_copy.wait()
            x_out_copy.start()
            for k in (0, 1):
                x_swap(OWN, k).start()
            y_first(1, 0).wait_recv()
            y_swap(RIGHT, 0).start()
            y_first(0, 1).wait_recv()
            y_swap(LEFT, 1).start()

        @pl.when(s == 6)
        def _():
            x_out_copy.wait()
            for k in (0, 1):
                y_second(k).wait_recv()
                y_swap(FAR, k).start()

        @pl.when(s == 7)
        def _():
            for d in (0, 1):
                x_first(d, d).wait_recv()
                x_second(d).start()
                x_swap((LEFT, RIGHT)[d], d).start()

        @pl.when(jnp.logical_or(s == 0, plane == 1))
        def _():
            for h in (0, 1):
                pltpu.make_async_copy(gy_hbm.at[half_of(h)], gy.at[s, half_of(h)], yr.at[s, h]).wait()

        for c in load_u(s, b):
            c.wait()

        @pl.when(s >= 2)
        def _():
            for c in store_u(s - 2, b):
                c.wait()

        for f in range(2):
            lines = pl.ds(f * (ffn // 2), ffn // 2)
            grad_h = dot_cols(wd[lines, :], gy[s])
            gate_f = ug[b, lines, :].astype(F32)
            up_f = uu[b, lines, :].astype(F32)
            sig_gate = jax.nn.sigmoid(gate_f)
            act_gate = gate_f * sig_gate
            silu_grad = sig_gate * (1.0 + gate_f * (1.0 - sig_gate))
            z[lines, :] = (act_gate * up_f).astype(BF16)
            duu[b, lines, :] = (grad_h * act_gate).astype(BF16)
            dug[b, lines, :] = (grad_h * up_f * silu_grad).astype(BF16)

        for c in store_u(s, b):
            c.start()
        accumulate(z, gy.at[s])
        to = plane * s + (1 - plane) * (part + slot)
        for h in (0, 1):
            buf[to, half_of(h), :] = (dot_rows(dug[b, :, half_of(h)], wg[...])
                                      + dot_rows(duu[b, :, half_of(h)], wu[...])).astype(BF16)

        @pl.when(plane == 1)
        def _():
            remote(buf.at[s], prec.at[slot], ps.at[slot], pr.at[slot], other).start()

        return carry

    lax.fori_loop(0, 8, unit, 0)
    gw_copies[0].start()

    def add_into(slot, row, src, at, count):
        step = 64

        def body(i, carry):
            to = pl.ds(pl.multiple_of(row + i * step, step), step)
            frm = pl.ds(pl.multiple_of(at + i * step, step), step)
            buf[slot, to, :] = (buf[slot, to, :].astype(F32) + src[frm, :].astype(F32)).astype(BF16)
            return carry

        lax.fori_loop(0, count // step, body, 0)

    p_swap(FAR).wait_recv()
    for d in (0, 1):
        add_into(part + FAR, d * half, prec.at[FAR], d * half, half)
        r_first(d).start()
    for d, slot in ((0, RIGHT), (1, LEFT)):
        p_swap(slot).wait_recv()
        add_into(part + slot, (1 - d) * half, prec.at[slot], (1 - d) * half, half)
        r_last(d, 1 - d).start()
    for d, slot in ((0, RIGHT), (1, LEFT)):
        add_into(part + slot, d * half, prec.at[slot], d * half, half)
    p_swap(OWN).wait_recv()
    add_into(part + OWN, 0, prec.at[OWN], 0, rows)
    for s in (6, 7):
        for c in store_u(s, s % 2):
            c.wait()
    for d in (0, 1):
        x_first(d, 1 - d).wait_recv()
        x_swap((LEFT, RIGHT)[d], 1 - d).start()
    p_swap(OWN).wait_send()
    p_swap(RIGHT).wait_send()
    for h in (0, 1):
        for slot in range(3):
            x_swap(slot, h).wait_recv()

    def x_load(s, b):
        return pltpu.make_async_copy(x_all.at[pl.ds(pl.multiple_of(s * rows, rows), rows)], buf.at[1 + 2 * b],
                                     u_sem.at[b, 0])

    def d_load(src, s, b):
        return pltpu.make_async_copy(src.at[:, pl.ds(pl.multiple_of(s * rows, rows), rows)], dug.at[b],
                                     u_sem.at[b, 1])

    def start_loads(t):
        b = lax.rem(t, 2)
        x_load(lax.rem(t, 8), b).start()

        @pl.when(t < 8)
        def _():
            d_load(dug_all, t, b).start()

        @pl.when(t >= 8)
        def _():
            d_load(duu_all, t - 8, b).start()

    start_loads(0)
    gw_copies[0].wait()
    clear()

    def step_w(t, carry):
        b = lax.rem(t, 2)

        @pl.when(t == 5)
        def _():
            for d in (0, 1):
                x_second(d).wait_recv()
                x_swap(FAR, d).start()

        @pl.when(t == 6)
        def _():
            for h in (0, 1):
                x_swap(FAR, h).wait_recv()

        @pl.when(t + 1 < 16)
        def _():
            start_loads(t + 1)

        @pl.when(t == 8)
        def _():
            gw_copies[1].start()
            gw_copies[1].wait()
            clear()

        x_load(lax.rem(t, 8), b).wait()
        d_load(dug_all, lax.rem(t, 8), b).wait()
        accumulate(dug.at[b], buf.at[1 + 2 * b])
        return carry

    lax.fori_loop(0, 16, step_w, 0)
    gw_copies[2].start()

    norm_loads = (pltpu.make_async_copy(xin_hbm, buf.at[0], b_sem.at[0]),
                  pltpu.make_async_copy(gres_hbm, buf.at[1], b_sem.at[1]))
    for c in norm_loads:
        c.start()
    for h in (0, 1):
        y_swap(RIGHT, h).wait_send()
    y_second(1).wait_send()
    for d in (0, 1):
        r_first(d).wait_recv()
    for q in range(4):
        for d, slot in ((0, RIGHT), (1, LEFT)):
            add_into(part + slot, d * half + q * quarter, hop.at[d], q * quarter, quarter)
            r_final(d, q).start()
    for c in norm_loads:
        c.wait()
    for d in (0, 1):
        r_last(d, 1 - d).wait_recv()
    step = 32
    gamma_f = gamma_ref[...].astype(F32).reshape(1, buf.shape[2])

    def norm_rows(row):
        def norm(i, carry):
            r = pl.ds(pl.multiple_of(row + i * step, step), step)
            grad_x = (buf[part, r, :].astype(F32) + fin[0, r, :].astype(F32) + fin[1, r, :].astype(F32)).astype(BF16)
            xin_f = buf[0, r, :].astype(F32)
            inv_rms = lax.rsqrt(jnp.mean(xin_f * xin_f, axis=-1, keepdims=True) + NORM_EPS)
            scaled = grad_x.astype(F32) * gamma_f
            proj_mean = jnp.mean(scaled * xin_f, axis=-1, keepdims=True)
            buf[2, r, :] = (buf[1, r, :].astype(F32)
                            + inv_rms * (scaled - xin_f * (inv_rms * inv_rms) * proj_mean)).astype(BF16)
            return carry

        lax.fori_loop(0, quarter // step, norm, 0)

    for q in range(4):
        for h in (0, 1):
            r_final(h, q).wait_recv()
            norm_rows(h * half + q * quarter)
            s_out(h, q).start()
            s_first(h, q).start()
            s_swap(h, q).start()

    for d in (0, 1):
        for h in (0, 1):
            y_first(d, h).wait_send()
            x_first(d, h).wait_send()
        r_last(d, 1 - d).wait_send()
        x_second(d).wait_send()
        r_first(d).wait_send()
    y_second(0).wait_send()
    for h in (0, 1):
        for slot in range(4):
            if slot != RIGHT:
                y_swap(slot, h).wait_send()
            x_swap(slot, h).wait_send()
        for q in range(4):
            r_final(h, q).wait_send()
            s_swap(h, q).wait_send()
            s_swap(h, q).wait_recv()
            s_out(h, q).wait()
            s_first(h, q).wait_send()
            s_first(h, q).wait_recv()
    for slot in (LEFT, FAR):
        p_swap(slot).wait_send()
    gw_copies[2].wait()


def settle_kernel(*refs):
    held, load_sem, store_sem = refs[-3:]
    arrays = (len(refs) - 3) // 2
    slots, lines = held.shape[0], held.shape[1]
    pieces = [(a, i) for a in range(arrays) for i in range(refs[a].shape[0] // lines)]
    lag = slots // 2

    def load(k):
        a, i = pieces[k]
        return pltpu.make_async_copy(refs[a].at[pl.ds(i * lines, lines)], held.at[k % slots], load_sem.at[k % slots])

    def store(k):
        a, i = pieces[k]
        return pltpu.make_async_copy(held.at[k % slots], refs[arrays + a].at[pl.ds(i * lines, lines)],
                                     store_sem.at[k % slots])

    for k in range(slots):
        load(k).start()
    for k in range(len(pieces)):
        if k >= lag:
            store(k - lag).wait()
            if k - lag + slots < len(pieces):
                load(k - lag + slots).start()
        load(k).wait()
        store(k).start()
    for k in range(len(pieces) - lag, len(pieces)):
        store(k).wait()


def tail_kernel(n, top, low, other_top, other_low, right_top, right_low, left_top, left_low, ot_hbm, wo_hbm,
                do_hbm, gwo_hbm,
                held, ot, wo, do, gwo, l_sem, o_sem, es, er, ss, sr, qs, qr):
    me = lax.axis_index("tp")
    core, chip, chips = lax.rem(me, 2), me // 2, n // 2
    right = lax.rem(chip + 1, chips) * 2 + core
    left = lax.rem(chip + chips - 1, chips) * 2 + core
    other = chip * 2 + 1 - core
    rows = held.shape[1]
    half = rows // 2
    quarter = half // 4
    halves = {0: (top, low), 1: (other_top, other_low), 2: (right_top, right_low), 4: (left_top, left_low)}

    def half_of(h):
        return pl.ds(h * half, half)

    def remote(src, dst, send, recv, to):
        return pltpu.make_async_remote_copy(src_ref=src, dst_ref=dst, send_sem=send, recv_sem=recv,
                                            device_id={"tp": to}, device_id_type=MESH)

    def second(d, q):
        return remote((left_top, right_low)[d].at[pl.ds(q * quarter, quarter)],
                      held.at[2 * FAR, pl.ds(d * half + q * quarter, quarter)], es.at[d, q], er.at[d, q],
                      (right, left)[d])

    def swap(slot, h):
        return remote(halves[2 * slot][h], held.at[2 * slot + 1, half_of(h)], ss.at[slot - 1, h], sr.at[slot - 1, h],
                      other)

    def far_swap(h, q):
        at = pl.ds(h * half + q * quarter, quarter)
        return remote(held.at[2 * FAR, at], held.at[2 * FAR + 1, at], qs.at[h, q], qr.at[h, q], other)

    def load(block, h):
        return pltpu.make_async_copy(halves[block][h], held.at[block, half_of(h)], l_sem.at[block, h])

    ot_copy = pltpu.make_async_copy(ot_hbm, ot, l_sem.at[3, 0])
    wo_copy = pltpu.make_async_copy(wo_hbm, wo, l_sem.at[3, 1])
    gwo_copy = pltpu.make_async_copy(gwo, gwo_hbm, o_sem.at[8])

    def do_out(block):
        at = lax.rem(chip + chip_step(block // 2), chips) * 2 + lax.rem(core + block % 2, 2)
        cols = pl.ds(pl.multiple_of(at * rows, rows), rows)
        return cols, pltpu.make_async_copy(do.at[:, cols], do_hbm.at[:, cols], o_sem.at[block])

    def process(block):
        cols, out = do_out(block)
        do[:, cols] = dot_cols(wo[...], held[block]).astype(BF16)
        out.start()
        share = jnp.dot(ot[:, cols], held[block], preferred_element_type=F32)
        gwo[...] = gwo[...] + share if block else share

    barrier = pltpu.get_barrier_semaphore()
    for peer in (right, left, other):
        pl.semaphore_signal(barrier, inc=1, device_id={"tp": peer}, device_id_type=MESH)
    wo_copy.start()
    for h in (0, 1):
        load(0, h).start()
    ot_copy.start()
    for block in (1, 2, 4):
        for h in (0, 1):
            load(block, h).start()
    pl.semaphore_wait(barrier, 3)
    for q in range(4):
        for d in (0, 1):
            second(d, q).start()
    for slot in (RIGHT, LEFT):
        for h in (0, 1):
            swap(slot, h).start()
    wo_copy.wait()
    ot_copy.wait()
    for block in (0, 1, 2, 4):
        for h in (0, 1):
            load(block, h).wait()
        process(block)
    for slot in (RIGHT, LEFT):
        for h in (0, 1):
            swap(slot, h).wait_recv()
        process(2 * slot + 1)
    for q in range(4):
        for h in (0, 1):
            second(h, q).wait_recv()
            far_swap(h, q).start()
    process(2 * FAR)
    for q in range(4):
        for h in (0, 1):
            far_swap(h, q).wait_recv()
    process(2 * FAR + 1)
    gwo_copy.start()
    for q in range(4):
        for h in (0, 1):
            second(h, q).wait_send()
            far_swap(h, q).wait_send()
    for slot in (RIGHT, LEFT):
        for h in (0, 1):
            swap(slot, h).wait_send()
    for block in range(8):
        do_out(block)[1].wait()
    gwo_copy.wait()


def solution(mesh):
    n = mesh.shape["tp"]
    chips = n // 2
    right_of = [(i, ((i // 2 + 1) % chips) * 2 + i % 2) for i in range(n)]
    left_of = [(i, ((i // 2 - 1) % chips) * 2 + i % 2) for i in range(n)]

    def go_right(a):
        return lax.ppermute(a, "tp", right_of)

    def go_left(a):
        return lax.ppermute(a, "tp", left_of)

    token_spec = P(("dp", "tp"), None)
    split_cols = P("dp", "tp")
    weight_cols = P(None, "tp")
    weight_rows = P("tp", None)

    def run_main(x_norm, grad_y, u_gate_t, u_up_t, w_gate_t, w_up_t, w_down, x_in, gamma, grad_res):
        rows, hidden = x_norm.shape
        ffn, tokens = u_gate_t.shape
        half = rows // 2
        any_spec = pl.BlockSpec(memory_space=pl.ANY)
        dma = pltpu.SemaphoreType.DMA
        return pl.pallas_call(
            functools.partial(main_kernel, n),
            out_shape=[jax.ShapeDtypeStruct(*a) for a in (
                ((tokens, hidden), BF16), ((ffn, tokens), BF16), ((ffn, tokens), BF16),
                ((ffn, hidden), F32), ((ffn, hidden), F32), ((ffn, hidden), F32),
                *[((half, hidden), BF16)] * 6)],
            in_specs=[any_spec] * 8 + [pl.BlockSpec(memory_space=pltpu.VMEM), any_spec],
            out_specs=[any_spec] * 12,
            scratch_shapes=[
                pltpu.VMEM((ffn, hidden), BF16), pltpu.VMEM((ffn, hidden), BF16), pltpu.VMEM((ffn, hidden), BF16),
                pltpu.VMEM((12, rows, hidden), BF16),
                pltpu.VMEM((2, ffn, rows), BF16), pltpu.VMEM((2, ffn, rows), BF16),
                pltpu.VMEM((ffn, rows), BF16), pltpu.VMEM((2, ffn, rows), BF16), pltpu.VMEM((2, ffn, rows), BF16),
                pltpu.VMEM((ffn, hidden), F32), pltpu.VMEM((4, rows, hidden), BF16),
                pltpu.VMEM((2, half, hidden), BF16), pltpu.VMEM((2, rows, hidden), BF16),
                dma((3,)), dma((2, 2)), dma((2, 4)), dma((2,)),
                dma((2, 3)), dma((4, 2)), dma((8, 2)),
                dma((2, 3)), dma((4, 2)), dma((8, 2)),
                dma((4,)), dma((4,)), dma((2,)), dma((2,)), dma((2, 2)), dma((2, 2)),
                dma((2, 4)), dma((2, 4)), dma((2, 4)), dma((2, 4)), dma((2, 4)),
                dma((2, 4)), dma((2, 4)),
            ],
            compiler_params=pltpu.CompilerParams(collective_id=0, has_side_effects=True,
                                                 vmem_limit_bytes=67_000_000),
        )(x_norm, grad_y, u_gate_t, u_up_t, w_gate_t, w_up_t, w_down, x_in, gamma, grad_res)

    any_space = pl.BlockSpec(memory_space=pl.ANY)

    def settle(*arrays):
        lines, hidden = arrays[0].shape
        slots = 8
        return pl.pallas_call(
            settle_kernel,
            in_specs=[any_space] * len(arrays), out_specs=[any_space] * len(arrays),
            out_shape=[jax.ShapeDtypeStruct(a.shape, a.dtype) for a in arrays],
            scratch_shapes=[pltpu.VMEM((slots, lines // 5, hidden), F32), pltpu.SemaphoreType.DMA((slots,)),
                            pltpu.SemaphoreType.DMA((slots,))],
            cost_estimate=pl.CostEstimate(flops=6000 * lines * hidden, bytes_accessed=24 * lines * hidden,
                                          transcendentals=0),
        )(*arrays)

    def run_tail(halves, attn_t, w_out):
        (half, hidden), (width, tokens) = halves[0].shape, attn_t.shape
        dma = pltpu.SemaphoreType.DMA
        return pl.pallas_call(
            functools.partial(tail_kernel, n),
            in_specs=[any_space] * 10, out_specs=[any_space] * 2,
            out_shape=[jax.ShapeDtypeStruct((width, tokens), BF16), jax.ShapeDtypeStruct((width, hidden), F32)],
            scratch_shapes=[
                pltpu.VMEM((8, 2 * half, hidden), BF16), pltpu.VMEM((width, tokens), BF16),
                pltpu.VMEM((width, hidden), BF16), pltpu.VMEM((width, tokens), BF16), pltpu.VMEM((width, hidden), F32),
                dma((5, 2)), dma((9,)), dma((2, 4)), dma((2, 4)), dma((2, 2)), dma((2, 2)), dma((2, 4)), dma((2, 4))],
            compiler_params=pltpu.CompilerParams(collective_id=1, has_side_effects=True),
        )(*halves, attn_t, w_out)

    def local_backward(x_norm, grad_y, u_gate, u_up, w_gate, w_up, w_down, x_in, gamma, grad_res, attn_out, w_out):
        _, _, _, gate_t, up_t, down, top, low, other_top, other_low, left_top, right_low = run_main(
            x_norm, grad_y, u_gate.T, u_up.T, w_gate.T, w_up.T, w_down, x_in, gamma, grad_res)

        left_low = go_right(low)
        right_top = go_left(top)
        gate_t, up_t, gw_down = settle(gate_t, up_t, down)
        grad_sum = jnp.concatenate([top, low], axis=0)
        do_t, gwo = run_tail((top, low, other_top, other_low, right_top, right_low, left_top, left_low),
                             attn_out.T, w_out)
        return grad_sum, do_t.T, gate_t.T, up_t.T, gw_down, gwo

    return jax.shard_map(
        local_backward,
        mesh=mesh,
        in_specs=(token_spec, token_spec, split_cols, split_cols, weight_cols, weight_cols, weight_rows,
                  token_spec, P(None), token_spec, split_cols, weight_rows),
        out_specs=(token_spec, split_cols, split_cols, split_cols, token_spec, token_spec),
        check_vma=False,
    )
```

profile of v0, /device:TPU:113, one launch (start us, length us, event | category | flops | bytes accessed | tf_op | source)
XLA Modules:
  0.0 228.7 jit_solution(15064487354280051752)
XLA Ops:
  0.6 177.1 %shard_map.163 = (bf16[4096,1536]{1,0:T(8,128)(2,1)}, bf16[1120,4096]{1,0:T(8,128)(2,1)}, bf16[1120,4096]{1,0:T(8,128)(2,1)}, f32[1120,1536]{1,0:T(8,128)}, f32[...) custom-call(bf16[512,1536]{1,0:T(8,128)(2,1)} %x_hbm.1, ...), custom_call_target="tpu_custom_call" | custom-call | tf_op jit(solution)/shard_map/pallas_call | solution.py:564
  177.8 1.2 collective-permute-start
  179.0 0.3 collective-permute-start.1
  179.3 2.6 %pad_maximum_fusion = bf16[512,1536]{1,0:T(8,128)(2,1)} fusion(bf16[256,1536]{1,0:T(8,128)(2,1)} %get-tuple-element.21.low, bf16[256,1536]{1,0:T(8,128)(2,1)} %get-tuple-element.20.top), kind=kLoop, calls=%fused_computation | loop fusion | flops 3145728 | bytes 3145728 | tf_op jit(solution)/shard_map/concatenate | solution.py:626
  181.9 14.6 %shard_map.165 = (f32[1120,1536]{1,0:T(8,128)}, f32[1120,1536]{1,0:T(8,128)}, f32[1120,1536]{1,0:T(8,128)}) custom-call(f32[1120,1536]{1,0:T(8,128)} %get-tuple-element.27.refs_0_, f32[1120,1536]{1,0:T(8,128)} %get-tuple-element.28.refs_1_, f32[1120,1536]{1,0:T(8,128)} %get-tuple-element.29.refs_2_), custom_call_target="tpu_custom_call" | custom-call | flops 10321920000 | bytes 41287680 | tf_op jit(solution)/shard_map/pallas_call | solution.py:595
  196.5 1.0 collective-permute-done.right_top
  197.5 0.0 copy-start.1
  197.5 1.3 collective-permute-done.1.left_low
  198.9 0.0 copy-start.2
  198.9 0.0 copy-done.1
  198.9 0.9 copy-done.2
  199.7 25.1 %shard_map.164 = (bf16[192,4096]{1,0:T(8,128)(2,1)}, f32[192,1536]{1,0:T(8,128)}) custom-call(bf16[256,1536]{1,0:T(8,128)(2,1)} %get-tuple-element.20.top, bf16[256,1536]{1,0:T(8,128)(2,1)} %get-tuple-element.21.low, bf16[256,1536]{1,0:T(8,128)(2,1)} %get-tuple-element.22.other_top, bf16[256,1536]{1,0:T(8,128)(2,1)} %get-tuple-element.23.other_low, ...), custom_call_target="tpu_custom_call" | custom-call | tf_op jit(solution)/shard_map/pallas_call | solution.py:608
  224.9 0.0 copy-start
  224.9 2.8 %copy.20 = bf16[4096,192]{0,1:T(8,128)(2,1)} copy(bf16[4096,192]{0,1:T(8,128)(2,1)} %bitcast.13) | data formatting | bytes 3145728
  227.7 0.0 copy-done
  227.7 1.0 copy.21
Async XLA Ops:
  177.8 19.7 %collective-permute-start = (bf16[256,1536]{1,0:T(8,128)(2,1)}, bf16[256,1536]{1,0:T(8,128)(2,1)S(1)}, u32[]{:S(2)}, u32[]{:S(2)}) collective-permute-start(bf16[256,1536]{1,0:T(8,128)(2,1)} %get-tuple-element.20.top), channel_id=1, source_target_pairs={{0,6},{1,7},{2,0},{3,1},{4,2},{5,3},{6,4},{7,5},{8,14},{9,15},{10,... | collective-permute-start | bytes 2359304 | tf_op jit(solution)/shard_map/ppermute | solution.py:551
  179.0 19.9 %collective-permute-start.1 = (bf16[256,1536]{1,0:T(8,128)(2,1)}, bf16[256,1536]{1,0:T(8,128)(2,1)S(1)}, u32[]{:S(2)}, u32[]{:S(2)}) collective-permute-start(bf16[256,1536]{1,0:T(8,128)(2,1)} %get-tuple-element.21.low), channel_id=1, source_target_pairs={{0,2},{1,3},{2,4},{3,5},{4,6},{5,7},{6,0},{7,1},{8,10},{9,11},{10,... | collective-permute-start | bytes 2359304 | tf_op jit(solution)/shard_map/ppermute | solution.py:548
  197.5 1.4 copy-start.1
  198.9 0.9 copy-start.2
  224.9 2.8 %copy-start = (f32[192,1536]{1,0:T(8,128)S(1)}, f32[192,1536]{1,0:T(8,128)}, u32[]{:S(2)}) copy-start(f32[192,1536]{1,0:T(8,128)} %get-tuple-element.45) | copy-start | bytes 3538948
where the time goes:
time: 229 us
  Pallas kernels  217 us (95%)
  local copies, waits for them, and re-layouts  4.69 us (2%)
  other arithmetic  2.61 us (1%)
  waiting for transfers between devices  2.35 us (1%)
    pallas_call x1, Pallas kernels, run_main(): pl.pallas_call(functools.partial(main_kernel, n), out_shape=[jax.ShapeDty...  177 us
    pallas_call x1, Pallas kernels, run_tail(): pl.pallas_call(functools.partial(tail_kernel, n), in_specs=[any_space] *...  25.1 us
    pallas_call x1, Pallas kernels, settle(): pl.pallas_call(settle_kernel, in_specs=[any_space] * len(arrays), out_spe...  14.6 us
    unnamed x8, local copies, waits for them, and re-layouts  4.69 us
  transfers between devices with their start and end apart: 2, of which 2 were waited for; matrix products, arithmetic and copies ran while one was open for 1% of the time, Pallas kernels for 6%

commit v1 on v0

--- a/solution.py
+++ b/solution.py
@@ -437,111 +437,61 @@
         store(k).wait()
 
 
-def tail_kernel(n, top, low, other_top, other_low, right_top, right_low, left_top, left_low, ot_hbm, wo_hbm,
-                do_hbm, gwo_hbm,
-                held, ot, wo, do, gwo, l_sem, o_sem, es, er, ss, sr, qs, qr):
+def attn_kernel(n, slots, *refs):
+    chunks = len(slots)
+    halves = refs[:4 * chunks]
+    held, ot, wo, do, gwo, h_sem, l_sem, o_sem = refs[-8:]
+    rest = refs[4 * chunks:-8]
+    ot_hbm, wo_hbm = rest[:2]
+    do_hbm, gwo_hbm = rest[-2:]
     me = lax.axis_index("tp")
     core, chip, chips = lax.rem(me, 2), me // 2, n // 2
-    right = lax.rem(chip + 1, chips) * 2 + core
-    left = lax.rem(chip + chips - 1, chips) * 2 + core
-    other = chip * 2 + 1 - core
     rows = held.shape[1]
     half = rows // 2
-    quarter = half // 4
-    halves = {0: (top, low), 1: (other_top, other_low), 2: (right_top, right_low), 4: (left_top, left_low)}
-
-    def half_of(h):
-        return pl.ds(h * half, half)
-
-    def remote(src, dst, send, recv, to):
-        return pltpu.make_async_remote_copy(src_ref=src, dst_ref=dst, send_sem=send, recv_sem=recv,
-                                            device_id={"tp": to}, device_id_type=MESH)
-
-    def second(d, q):
-        return remote((left_top, right_low)[d].at[pl.ds(q * quarter, quarter)],
-                      held.at[2 * FAR, pl.ds(d * half + q * quarter, quarter)], es.at[d, q], er.at[d, q],
-                      (right, left)[d])
-
-    def swap(slot, h):
-        return remote(halves[2 * slot][h], held.at[2 * slot + 1, half_of(h)], ss.at[slot - 1, h], sr.at[slot - 1, h],
-                      other)
-
-    def far_swap(h, q):
-        at = pl.ds(h * half + q * quarter, quarter)
-        return remote(held.at[2 * FAR, at], held.at[2 * FAR + 1, at], qs.at[h, q], qr.at[h, q], other)
-
-    def load(block, h):
-        return pltpu.make_async_copy(halves[block][h], held.at[block, half_of(h)], l_sem.at[block, h])
-
-    ot_copy = pltpu.make_async_copy(ot_hbm, ot, l_sem.at[3, 0])
-    wo_copy = pltpu.make_async_copy(wo_hbm, wo, l_sem.at[3, 1])
-    gwo_copy = pltpu.make_async_copy(gwo, gwo_hbm, o_sem.at[8])
-
-    def do_out(block):
-        at = lax.rem(chip + chip_step(block // 2), chips) * 2 + lax.rem(core + block % 2, 2)
-        cols = pl.ds(pl.multiple_of(at * rows, rows), rows)
-        return cols, pltpu.make_async_copy(do.at[:, cols], do_hbm.at[:, cols], o_sem.at[block])
-
-    def process(block):
-        cols, out = do_out(block)
-        do[:, cols] = dot_cols(wo[...], held[block]).astype(BF16)
-        out.start()
-        share = jnp.dot(ot[:, cols], held[block], preferred_element_type=F32)
-        gwo[...] = gwo[...] + share if block else share
-
-    barrier = pltpu.get_barrier_semaphore()
-    for peer in (right, left, other):
-        pl.semaphore_signal(barrier, inc=1, device_id={"tp": peer}, device_id_type=MESH)
-    wo_copy.start()
-    for h in (0, 1):
-        load(0, h).start()
-    ot_copy.start()
-    for block in (1, 2, 4):
-        for h in (0, 1):
-            load(block, h).start()
-    pl.semaphore_wait(barrier, 3)
-    for q in range(4):
-        for d in (0, 1):
-            second(d, q).start()
-    for slot in (RIGHT, LEFT):
-        for h in (0, 1):
-            swap(slot, h).start()
-    wo_copy.wait()
-    ot_copy.wait()
-    for block in (0, 1, 2, 4):
-        for h in (0, 1):
-            load(block, h).wait()
-        process(block)
-    for slot in (RIGHT, LEFT):
-        for h in (0, 1):
-            swap(slot, h).wait_recv()
-        process(2 * slot + 1)
-    for q in range(4):
-        for h in (0, 1):
-            second(h, q).wait_recv()
-            far_swap(h, q).start()
-    process(2 * FAR)
-    for q in range(4):
-        for h in (0, 1):
-            far_swap(h, q).wait_recv()
-    process(2 * FAR + 1)
-    gwo_copy.start()
-    for q in range(4):
-        for h in (0, 1):
-            second(h, q).wait_send()
-            far_swap(h, q).wait_send()
-    for slot in (RIGHT, LEFT):
-        for h in (0, 1):
-            swap(slot, h).wait_send()
-    for block in range(8):
-        do_out(block)[1].wait()
-    gwo_copy.wait()
+    loads = [pltpu.make_async_copy(src, held.at[k // 2, pl.ds(k % 2 * half, half)], h_sem.at[k])
+             for k, src in enumerate(halves)]
+
+    def place(block):
+        there = lax.rem(chip + chip_step(slots[block // 2]), chips) * 2 + lax.rem(core + block % 2, 2)
+        return pl.ds(pl.multiple_of(there * rows, rows), rows)
+
+    wo_load = pltpu.make_async_copy(wo_hbm, wo, l_sem.at[0])
+    gwo_load = None if slots[0] == OWN else pltpu.make_async_copy(rest[2], gwo, l_sem.at[1])
+    ots = [pltpu.make_async_copy(ot_hbm.at[:, place(b)], ot.at[b], l_sem.at[2 + b]) for b in range(2 * chunks)]
+    wo_load.start()
+    for b in range(2 * chunks):
+        loads[2 * b].start()
+        loads[2 * b + 1].start()
+        ots[b].start()
+        if b == 0 and gwo_load is not None:
+            gwo_load.start()
+    wo_load.wait()
+    outs = []
+    for b in range(2 * chunks):
+        loads[2 * b].wait()
+        loads[2 * b + 1].wait()
+        if slots[0] == OWN and b == 0:
+            outs.append(pltpu.make_async_copy(held.at[0], rest[2], o_sem.at[2 * chunks + 1]))
+            outs[-1].start()
+        do[b] = dot_cols(wo[...], held[b]).astype(BF16)
+        outs.append(pltpu.make_async_copy(do.at[b], do_hbm.at[:, place(b)], o_sem.at[b]))
+        outs[-1].start()
+        ots[b].wait()
+        if b == 0 and gwo_load is not None:
+            gwo_load.wait()
+        share = jnp.dot(ot[b], held[b], preferred_element_type=F32)
+        gwo[...] = share if slots[b // 2] == OWN and b == 0 else gwo[...] + share
+    outs.append(pltpu.make_async_copy(gwo, gwo_hbm, o_sem.at[2 * chunks]))
+    outs[-1].start()
+    for c in outs:
+        c.wait()
 
 
 def solution(mesh):
     n = mesh.shape["tp"]
     chips = n // 2
     right_of = [(i, ((i // 2 + 1) % chips) * 2 + i % 2) for i in range(n)]
+    partner_of = [(i, i ^ 1) for i in range(n)]
     left_of = [(i, ((i // 2 - 1) % chips) * 2 + i % 2) for i in range(n)]
 
     def go_right(a):
@@ -549,6 +499,9 @@
 
     def go_left(a):
         return lax.ppermute(a, "tp", left_of)
+
+    def swap(a):
+        return lax.ppermute(a, "tp", partner_of)
 
     token_spec = P(("dp", "tp"), None)
     split_cols = P("dp", "tp")
@@ -591,41 +544,58 @@
 
     def settle(*arrays):
         lines, hidden = arrays[0].shape
-        slots = 8
+        slots = min(16, 10 * len(arrays))
         return pl.pallas_call(
             settle_kernel,
             in_specs=[any_space] * len(arrays), out_specs=[any_space] * len(arrays),
             out_shape=[jax.ShapeDtypeStruct(a.shape, a.dtype) for a in arrays],
-            scratch_shapes=[pltpu.VMEM((slots, lines // 5, hidden), F32), pltpu.SemaphoreType.DMA((slots,)),
+            scratch_shapes=[pltpu.VMEM((slots, lines // 10, hidden), F32), pltpu.SemaphoreType.DMA((slots,)),
                             pltpu.SemaphoreType.DMA((slots,))],
-            cost_estimate=pl.CostEstimate(flops=6000 * lines * hidden, bytes_accessed=24 * lines * hidden,
+            cost_estimate=pl.CostEstimate(flops=2000 * len(arrays) * lines * hidden,
+                                          bytes_accessed=8 * len(arrays) * lines * hidden, transcendentals=0),
+            compiler_params=pltpu.CompilerParams(vmem_limit_bytes=67_000_000),
+        )(*arrays)
+
+    def attn(slots, halves, attn_t, w_out, *sofar):
+        (half, hidden), (width, tokens) = halves[0].shape, attn_t.shape
+        blocks = 2 * len(slots)
+        dma = pltpu.SemaphoreType.DMA
+        results = [jax.ShapeDtypeStruct((width, tokens), BF16), jax.ShapeDtypeStruct((width, hidden), F32)]
+        if not sofar:
+            results.insert(0, jax.ShapeDtypeStruct((2 * half, hidden), BF16))
+        return pl.pallas_call(
+            functools.partial(attn_kernel, n, slots),
+            in_specs=[any_space] * (2 * blocks + 2 + len(sofar)), out_specs=[any_space] * len(results),
+            scratch_shapes=[
+                pltpu.VMEM((blocks, 2 * half, hidden), BF16), pltpu.VMEM((blocks, width, 2 * half), BF16),
+                pltpu.VMEM((width, hidden), BF16), pltpu.VMEM((blocks, width, 2 * half), BF16),
+                pltpu.VMEM((width, hidden), F32), dma((2 * blocks,)), dma((2 + blocks,)), dma((2 + blocks,))],
+            out_shape=results,
+            input_output_aliases={2 * blocks + 3: 0} if sofar else {},
+            cost_estimate=pl.CostEstimate(flops=600 * blocks * half * hidden, bytes_accessed=8 * blocks * half * hidden,
                                           transcendentals=0),
-        )(*arrays)
-
-    def run_tail(halves, attn_t, w_out):
-        (half, hidden), (width, tokens) = halves[0].shape, attn_t.shape
-        dma = pltpu.SemaphoreType.DMA
-        return pl.pallas_call(
-            functools.partial(tail_kernel, n),
-            in_specs=[any_space] * 10, out_specs=[any_space] * 2,
-            out_shape=[jax.ShapeDtypeStruct((width, tokens), BF16), jax.ShapeDtypeStruct((width, hidden), F32)],
-            scratch_shapes=[
-                pltpu.VMEM((8, 2 * half, hidden), BF16), pltpu.VMEM((width, tokens), BF16),
-                pltpu.VMEM((width, hidden), BF16), pltpu.VMEM((width, tokens), BF16), pltpu.VMEM((width, hidden), F32),
-                dma((5, 2)), dma((9,)), dma((2, 4)), dma((2, 4)), dma((2, 2)), dma((2, 2)), dma((2, 4)), dma((2, 4))],
-            compiler_params=pltpu.CompilerParams(collective_id=1, has_side_effects=True),
-        )(*halves, attn_t, w_out)
+            compiler_params=pltpu.CompilerParams(vmem_limit_bytes=67_000_000),
+        )(*halves, attn_t, w_out, *sofar)
 
     def local_backward(x_norm, grad_y, u_gate, u_up, w_gate, w_up, w_down, x_in, gamma, grad_res, attn_out, w_out):
+        attn_t = attn_out.T
         _, _, _, gate_t, up_t, down, top, low, other_top, other_low, left_top, right_low = run_main(
             x_norm, grad_y, u_gate.T, u_up.T, w_gate.T, w_up.T, w_down, x_in, gamma, grad_res)
 
         left_low = go_right(low)
         right_top = go_left(top)
-        gate_t, up_t, gw_down = settle(gate_t, up_t, down)
-        grad_sum = jnp.concatenate([top, low], axis=0)
-        do_t, gwo = run_tail((top, low, other_top, other_low, right_top, right_low, left_top, left_low),
-                             attn_out.T, w_out)
+        left_top_other, right_low_other = swap(left_top), swap(right_low)
+        gate_t, up_t = settle(gate_t, up_t)
+        far_top = go_right(left_top)
+        far_low = go_left(right_low)
+        grad_sum, do_t, gwo = attn((OWN,), (top, low, other_top, other_low), attn_t, w_out)
+        left_low_other, right_top_other = swap(left_low), swap(right_top)
+        gw_down, = settle(down)
+        do_t, gwo = attn((RIGHT, LEFT), (
+            right_top, right_low, right_top_other, right_low_other,
+            left_top, left_low, left_top_other, left_low_other), attn_t, w_out, gwo, do_t)
+        far = (far_top, far_low, swap(far_top), swap(far_low))
+        do_t, gwo = attn((FAR,), far, attn_t, w_out, gwo, do_t)
         return grad_sum, do_t.T, gate_t.T, up_t.T, gw_down, gwo
 
     return jax.shard_map(

time: 229 us -> 250 us (1.092)
  waiting for transfers between devices: 2.35 us -> 30.1 us
  starting transfers between devices: 1.54 us -> 9.44 us
  Pallas kernels: 217 us -> 210 us
  local copies, waits for them, and re-layouts: 4.69 us -> 0 us
  other arithmetic: 2.61 us -> 0 us
    ppermute x1 -> x2, waiting for transfers between devices: 1 us -> 15.1 us  [go_left(): return lax.ppermute(a, 'tp', left_of)]
    ppermute x1 -> x2, waiting for transfers between devices: 1.35 us -> 15 us  [go_right(): return lax.ppermute(a, 'tp', right_of)]
    pallas_call x1 -> x3, Pallas kernels: 25.1 us -> 16.9 us  [attn(): pl.pallas_call(functools.partial(attn_kernel, n, slots), in_specs=[any_sp...]
    ppermute x0 -> x6, starting transfers between devices: none -> 4.94 us  [swap(): return lax.ppermute(a, 'tp', partner_of)]
    unnamed x8 -> x0, local copies, waits for them, and re-layouts: 4.69 us -> none
    concatenate x1 -> x0, other arithmetic: 2.61 us -> none  [local_backward(): grad_sum = jnp.concatenate([top, low], axis=0)]
    pallas_call x1 -> x2, Pallas kernels: 14.6 us -> 15.8 us  [settle(): pl.pallas_call(settle_kernel, in_specs=[any_space] * len(arrays), out_spe...]
  transfers between devices with their start and end apart: 2 -> 10, of which waited for: 2 -> 3; matrix products, arithmetic and copies ran while one was open for 1% -> 0% of each run, Pallas kernels for 6% -> 11%
where the time goes in v1:
time: 250 us
  Pallas kernels  210 us (84%)
  waiting for transfers between devices  30.1 us (12%)
  starting transfers between devices  9.44 us (4%)
    pallas_call x1, Pallas kernels, run_main(): pl.pallas_call(functools.partial(main_kernel, n), out_shape=[jax.ShapeDty...  177 us
    pallas_call x3, Pallas kernels, attn(): pl.pallas_call(functools.partial(attn_kernel, n, slots), in_specs=[any_sp...  16.9 us
    pallas_call x2, Pallas kernels, settle(): pl.pallas_call(settle_kernel, in_specs=[any_space] * len(arrays), out_spe...  15.8 us
    ppermute x2, waiting for transfers between devices, go_left(): return lax.ppermute(a, 'tp', left_of)  15.1 us
    ppermute x2, waiting for transfers between devices, go_right(): return lax.ppermute(a, 'tp', right_of)  15 us
  transfers between devices with their start and end apart: 10, of which 3 were waited for; matrix products, arithmetic and copies ran while one was open for 0% of the time, Pallas kernels for 11%

profile of v1, /device:TPU:113, one launch (start us, length us, event | category | flops | bytes accessed | tf_op | source)
XLA Modules:
  0.0 250.3 jit_solution(13296675113277749768)
XLA Ops:
  0.6 177.1 %shard_map.163 = (bf16[4096,1536]{1,0:T(8,128)(2,1)}, bf16[1120,4096]{1,0:T(8,128)(2,1)}, bf16[1120,4096]{1,0:T(8,128)(2,1)}, f32[1120,1536]{1,0:T(8,128)}, f32[...) custom-call(bf16[512,1536]{1,0:T(8,128)(2,1)} %x_hbm.1, ...), custom_call_target="tpu_custom_call" | custom-call | tf_op jit(solution)/shard_map/pallas_call | solution.py:517
  177.8 1.2 collective-permute-start.4
  179.0 0.3 collective-permute-start.7
  179.3 0.3 collective-permute-start.8
  179.6 0.6 collective-permute-start
  180.2 2.3 collective-permute-start.1
  182.6 15.1 %collective-permute-done.4.refs_0_ = bf16[256,1536]{1,0:T(8,128)(2,1)} collective-permute-done((bf16[256,1536]{1,0:T(8,128)(2,1)}, bf16[256,1536]{1,0:T(8,128)(2,1)}, u32[]{:S(2)}, u32[]{:S(2)}) %collective-permute-start.4) | collective-permute-done | bytes 786464 | tf_op jit(solution)/shard_map/ppermute | solution.py:501
  197.6 0.6 collective-permute-start.6
  198.2 0.7 collective-permute-done.7.refs_5_
  199.0 2.6 %collective-permute-start.5 = (bf16[256,1536]{1,0:T(8,128)(2,1)}, bf16[256,1536]{1,0:T(8,128)(2,1)}, u32[]{:S(2)}, u32[]{:S(2)}) collective-permute-start(bf16[256,1536]{1,0:T(8,128)(2,1)} %collective-permute-done.4.refs_0_), channel_id=1, source_target_pairs={{0,1},{1,0},{2,3},{3,2},{4,5},{5,4},{6,7},{7,6},{8,9},{9,8},{10,11... | collective-permute-start | bytes 2359304 | tf_op jit(solution)/shard_map/ppermute | solution.py:504
  201.5 0.0 collective-permute-done.8.refs_6_
  201.5 0.0 collective-permute-start.9
  201.5 14.3 %collective-permute-done.refs_0_ = bf16[256,1536]{1,0:T(8,128)(2,1)} collective-permute-done((bf16[256,1536]{1,0:T(8,128)(2,1)}, bf16[256,1536]{1,0:T(8,128)(2,1)}, u32[]{:S(2)}, u32[]{:S(2)}) %collective-permute-start) | collective-permute-done | bytes 786464 | tf_op jit(solution)/shard_map/ppermute | solution.py:498
  215.8 1.5 collective-permute-start.2
  217.3 0.0 collective-permute-done.1.refs_1_
  217.3 0.0 collective-permute-start.3
  217.3 5.7 %shard_map.168 = f32[1120,1536]{1,0:T(8,128)} custom-call(f32[1120,1536]{1,0:T(8,128)} %get-tuple-element.40.refs_0_), custom_call_target="tpu_custom_call" | custom-call | flops 3440640000 | bytes 13762560 | tf_op jit(solution)/shard_map/pallas_call | solution.py:548
  223.0 4.8 %shard_map.164 = (bf16[512,1536]{1,0:T(8,128)(2,1)}, bf16[192,4096]{1,0:T(8,128)(2,1)}, f32[192,1536]{1,0:T(8,128)}) custom-call(bf16[256,1536]{1,0:T(8,128)(2,1)} %get-tuple-element.24.refs_0_, bf16[256,1536]{1,0:T(8,128)(2,1)} %get-tuple-element.25.refs_1_, bf16[256,1536]{1,0:T(8,128)(2,1)} %get-tuple-element.26.refs_2_, ...), custom_call_target="tpu_custom_call" | custom-call | flops 471859200 | bytes 6291456 | tf_op jit(solution)/shard_map/pallas_call | solution.py:566
  227.9 10.0 %shard_map.167 = (f32[1120,1536]{1,0:T(8,128)}, f32[1120,1536]{1,0:T(8,128)}) custom-call(f32[1120,1536]{1,0:T(8,128)} %get-tuple-element.36.refs_0_, f32[1120,1536]{1,0:T(8,128)} %get-tuple-element.37.refs_1_), custom_call_target="tpu_custom_call" | custom-call | flops 6881280000 | bytes 27525120 | tf_op jit(solution)/shard_map/pallas_call | solution.py:548
  237.9 0.0 collective-permute-done.6.refs_3_
  237.9 0.0 collective-permute-done.5.refs_2_
  238.0 0.0 collective-permute-done.9.refs_7_
  238.0 7.2 %shard_map.165 = (bf16[192,4096]{1,0:T(8,128)(2,1)}, f32[192,1536]{1,0:T(8,128)}) custom-call(bf16[256,1536]{1,0:T(8,128)(2,1)} %collective-permute-done.4.refs_0_, bf16[256,1536]{1,0:T(8,128)(2,1)} %get-tuple-element.30.refs_1_, bf16[256,1536]{1,0:T(8,128)(2,1)} %collective-permute-done.5.refs_2_, ...), custom_call_target="tpu_custom_call", output_to_operand_aliasing={{0}: (11, {})} | custom-call | flops 943718400 | bytes 12582912 | tf_op jit(solution)/shard_map/pallas_call | solution.py:566
  245.2 0.0 collective-permute-done.2.refs_2_
  245.2 0.0 collective-permute-done.3.refs_3_
  245.2 4.9 %shard_map.166 = (bf16[192,4096]{1,0:T(8,128)(2,1)}, f32[192,1536]{1,0:T(8,128)}) custom-call(bf16[256,1536]{1,0:T(8,128)(2,1)} %collective-permute-done.refs_0_, bf16[256,1536]{1,0:T(8,128)(2,1)} %collective-permute-done.1.refs_1_, bf16[256,1536]{1,0:T(8,128)(2,1)} %collective-permute-done.2.refs_2_, ...), custom_call_target="tpu_custom_call", output_to_operand_aliasing={{0}: (7, {})} | custom-call | flops 471859200 | bytes 6291456 | tf_op jit(solution)/shard_map/pallas_call | solution.py:566
Async XLA Ops:
  177.8 19.8 %collective-permute-start.4 = (bf16[256,1536]{1,0:T(8,128)(2,1)}, bf16[256,1536]{1,0:T(8,128)(2,1)}, u32[]{:S(2)}, u32[]{:S(2)}) collective-permute-start(bf16[256,1536]{1,0:T(8,128)(2,1)} %get-tuple-element.24.refs_0_), channel_id=1, source_target_pairs={{0,6},{1,7},{2,0},{3,1},{4,2},{5,3},{6,4},{7,5},{8,14},{9,15},{10,... | collective-permute-start | bytes 2359304 | tf_op jit(solution)/shard_map/ppermute | solution.py:501
  179.0 20.0 %collective-permute-start.7 = (bf16[256,1536]{1,0:T(8,128)(2,1)}, bf16[256,1536]{1,0:T(8,128)(2,1)}, u32[]{:S(2)}, u32[]{:S(2)}) collective-permute-start(bf16[256,1536]{1,0:T(8,128)(2,1)} %get-tuple-element.25.refs_1_), channel_id=1, source_target_pairs={{0,2},{1,3},{2,4},{3,5},{4,6},{5,7},{6,0},{7,1},{8,10},{9,11},{10,... | collective-permute-start | bytes 2359304 | tf_op jit(solution)/shard_map/ppermute | solution.py:498
  179.3 22.2 %collective-permute-start.8 = (bf16[256,1536]{1,0:T(8,128)(2,1)}, bf16[256,1536]{1,0:T(8,128)(2,1)}, u32[]{:S(2)}, u32[]{:S(2)}) collective-permute-start(bf16[256,1536]{1,0:T(8,128)(2,1)} %get-tuple-element.29.refs_4_), channel_id=1, source_target_pairs={{0,1},{1,0},{2,3},{3,2},{4,5},{5,4},{6,7},{7,6},{8,9},{9,8},{10,11... | collective-permute-start | bytes 2359304 | tf_op jit(solution)/shard_map/ppermute | solution.py:504
  179.6 36.2 %collective-permute-start = (bf16[256,1536]{1,0:T(8,128)(2,1)}, bf16[256,1536]{1,0:T(8,128)(2,1)}, u32[]{:S(2)}, u32[]{:S(2)}) collective-permute-start(bf16[256,1536]{1,0:T(8,128)(2,1)} %get-tuple-element.29.refs_4_), channel_id=1, source_target_pairs={{0,2},{1,3},{2,4},{3,5},{4,6},{5,7},{6,0},{7,1},{8,10},{9,11},{10,... | collective-permute-start | bytes 2359304 | tf_op jit(solution)/shard_map/ppermute | solution.py:498
  180.2 37.1 %collective-permute-start.1 = (bf16[256,1536]{1,0:T(8,128)(2,1)}, bf16[256,1536]{1,0:T(8,128)(2,1)}, u32[]{:S(2)}, u32[]{:S(2)}) collective-permute-start(bf16[256,1536]{1,0:T(8,128)(2,1)} %get-tuple-element.30.refs_1_), channel_id=1, source_target_pairs={{0,6},{1,7},{2,0},{3,1},{4,2},{5,3},{6,4},{7,5},{8,14},{9,15},{10,... | collective-permute-start | bytes 2359304 | tf_op jit(solution)/shard_map/ppermute | solution.py:501
  197.6 40.3 %collective-permute-start.6 = (bf16[256,1536]{1,0:T(8,128)(2,1)}, bf16[256,1536]{1,0:T(8,128)(2,1)}, u32[]{:S(2)}, u32[]{:S(2)}) collective-permute-start(bf16[256,1536]{1,0:T(8,128)(2,1)} %get-tuple-element.30.refs_1_), channel_id=1, source_target_pairs={{0,1},{1,0},{2,3},{3,2},{4,5},{5,4},{6,7},{7,6},{8,9},{9,8},{10,11... | collective-permute-start | bytes 2359304 | tf_op jit(solution)/shard_map/ppermute | solution.py:504
  199.0 39.0 %collective-permute-start.5 = (bf16[256,1536]{1,0:T(8,128)(2,1)}, bf16[256,1536]{1,0:T(8,128)(2,1)}, u32[]{:S(2)}, u32[]{:S(2)}) collective-permute-start(bf16[256,1536]{1,0:T(8,128)(2,1)} %collective-permute-done.4.refs_0_), channel_id=1, source_target_pairs={{0,1},{1,0},{2,3},{3,2},{4,5},{5,4},{6,7},{7,6},{8,9},{9,8},{10,11... | collective-permute-start | bytes 2359304 | tf_op jit(solution)/shard_map/ppermute | solution.py:504
  201.5 36.4 %collective-permute-start.9 = (bf16[256,1536]{1,0:T(8,128)(2,1)}, bf16[256,1536]{1,0:T(8,128)(2,1)}, u32[]{:S(2)}, u32[]{:S(2)}) collective-permute-start(bf16[256,1536]{1,0:T(8,128)(2,1)} %collective-permute-done.7.refs_5_), channel_id=1, source_target_pairs={{0,1},{1,0},{2,3},{3,2},{4,5},{5,4},{6,7},{7,6},{8,9},{9,8},{10,11... | collective-permute-start | bytes 2359304 | tf_op jit(solution)/shard_map/ppermute | solution.py:504
  215.8 29.4 %collective-permute-start.2 = (bf16[256,1536]{1,0:T(8,128)(2,1)}, bf16[256,1536]{1,0:T(8,128)(2,1)}, u32[]{:S(2)}, u32[]{:S(2)}) collective-permute-start(bf16[256,1536]{1,0:T(8,128)(2,1)} %collective-permute-done.refs_0_), channel_id=1, source_target_pairs={{0,1},{1,0},{2,3},{3,2},{4,5},{5,4},{6,7},{7,6},{8,9},{9,8},{10,11... | collective-permute-start | bytes 2359304 | tf_op jit(solution)/shard_map/ppermute | solution.py:504
  217.3 27.9 %collective-permute-start.3 = (bf16[256,1536]{1,0:T(8,128)(2,1)}, bf16[256,1536]{1,0:T(8,128)(2,1)}, u32[]{:S(2)}, u32[]{:S(2)}) collective-permute-start(bf16[256,1536]{1,0:T(8,128)(2,1)} %collective-permute-done.1.refs_1_), channel_id=1, source_target_pairs={{0,1},{1,0},{2,3},{3,2},{4,5},{5,4},{6,7},{7,6},{8,9},{9,8},{10,11... | collective-permute-start | bytes 2359304 | tf_op jit(solution)/shard_map/ppermute | solution.py:504

commit v2 on v1

--- a/solution.py
+++ b/solution.py
@@ -29,7 +29,8 @@
 
 
 def main_kernel(n, x_hbm, gy_hbm, ug_hbm, uu_hbm, wg_hbm, wu_hbm, wd_hbm, xin_hbm, gamma_ref, gres_hbm,
-                x_all, dug_all, duu_all, gwg_hbm, gwu_hbm, gwd_hbm, ds_top, ds_low, other_top, other_low, left_top, right_low,
+                x_all, dug_all, duu_all, gwg_hbm, gwu_hbm, gwd_hbm, ds_top_a, ds_top_b, ds_low_a, ds_low_b,
+                other_top, other_low, left_top, right_low,
                 wg, wu, wd, buf, ug, uu, z, dug, duu, acc, prec, hop, fin,
                 w_sem, u_sem, o_sem, b_sem, ys, yd, yr, xs, xd, xr, ps, pr, hs, hr, fs, fr, qs, qr, ss, sr, ds_sem,
                 as_, ar):
@@ -124,7 +125,8 @@
 
     def s_out(h, q):
         return pltpu.make_async_copy(buf.at[2, pl.ds(h * half + q * quarter, quarter)],
-                                     (ds_top, ds_low)[h].at[pl.ds(q * quarter, quarter)], ds_sem.at[h, q])
+                                     ((ds_top_a, ds_top_b), (ds_low_a, ds_low_b))[h][q // 2].at[
+                                         pl.ds(q % 2 * quarter, quarter)], ds_sem.at[h, q])
 
     weights = [pltpu.make_async_copy(a, b, w_sem.at[i])
                for i, (a, b) in enumerate(((wd_hbm, wd), (wg_hbm, wg), (wu_hbm, wu)))]
@@ -437,51 +439,58 @@
         store(k).wait()
 
 
-def attn_kernel(n, slots, *refs):
-    chunks = len(slots)
-    halves = refs[:4 * chunks]
+def attn_kernel(n, pieces, rows, *refs):
+    count = len(pieces)
+    parts = refs[:count]
     held, ot, wo, do, gwo, h_sem, l_sem, o_sem = refs[-8:]
-    rest = refs[4 * chunks:-8]
+    rest = refs[count:-8]
     ot_hbm, wo_hbm = rest[:2]
     do_hbm, gwo_hbm = rest[-2:]
+    begins = pieces[0][0] == OWN
     me = lax.axis_index("tp")
     core, chip, chips = lax.rem(me, 2), me // 2, n // 2
-    rows = held.shape[1]
-    half = rows // 2
-    loads = [pltpu.make_async_copy(src, held.at[k // 2, pl.ds(k % 2 * half, half)], h_sem.at[k])
-             for k, src in enumerate(halves)]
-
-    def place(block):
-        there = lax.rem(chip + chip_step(slots[block // 2]), chips) * 2 + lax.rem(core + block % 2, 2)
-        return pl.ds(pl.multiple_of(there * rows, rows), rows)
-
+    ends = [sum(p.shape[0] for p in parts[:i + 1]) for i in range(count)]
+
+    def here(i):
+        return pl.ds(ends[i] - parts[i].shape[0], parts[i].shape[0])
+
+    def there(i):
+        slot, plane, row = pieces[i]
+        block = lax.rem(chip + chip_step(slot), chips) * 2 + lax.rem(core + plane, 2)
+        return pl.ds(pl.multiple_of(block * rows + row, 128), parts[i].shape[0])
+
+    loads = [(pltpu.make_async_copy(parts[i], held.at[here(i)], h_sem.at[i]),
+              pltpu.make_async_copy(ot_hbm.at[:, there(i)], ot.at[:, here(i)], l_sem.at[2 + i])) for i in range(count)]
     wo_load = pltpu.make_async_copy(wo_hbm, wo, l_sem.at[0])
-    gwo_load = None if slots[0] == OWN else pltpu.make_async_copy(rest[2], gwo, l_sem.at[1])
-    ots = [pltpu.make_async_copy(ot_hbm.at[:, place(b)], ot.at[b], l_sem.at[2 + b]) for b in range(2 * chunks)]
+    gwo_load = None if begins else pltpu.make_async_copy(rest[2], gwo, l_sem.at[1])
     wo_load.start()
-    for b in range(2 * chunks):
-        loads[2 * b].start()
-        loads[2 * b + 1].start()
-        ots[b].start()
-        if b == 0 and gwo_load is not None:
+    for i in range(count):
+        for c in loads[i]:
+            c.start()
+        if ends[i] == rows and gwo_load is not None:
             gwo_load.start()
     wo_load.wait()
     outs = []
-    for b in range(2 * chunks):
-        loads[2 * b].wait()
-        loads[2 * b + 1].wait()
-        if slots[0] == OWN and b == 0:
-            outs.append(pltpu.make_async_copy(held.at[0], rest[2], o_sem.at[2 * chunks + 1]))
+    done = 0
+    for low in range(0, ends[-1], rows):
+        first = done
+        while done < count and ends[done] <= low + rows:
+            for c in loads[done]:
+                c.wait()
+            done += 1
+        now = pl.ds(low, rows)
+        if begins and low == 0:
+            outs.append(pltpu.make_async_copy(held.at[now], rest[2], o_sem.at[count + 1]))
             outs[-1].start()
-        do[b] = dot_cols(wo[...], held[b]).astype(BF16)
-        outs.append(pltpu.make_async_copy(do.at[b], do_hbm.at[:, place(b)], o_sem.at[b]))
-        outs[-1].start()
-        ots[b].wait()
-        if b == 0 and gwo_load is not None:
+        do[:, now] = dot_cols(wo[...], held[now, :]).astype(BF16)
+        for i in range(first, done):
+            outs.append(pltpu.make_async_copy(do.at[:, here(i)], do_hbm.at[:, there(i)], o_sem.at[i]))
+            outs[-1].start()
+        if low == 0 and gwo_load is not None:
             gwo_load.wait()
-        share = jnp.dot(ot[b], held[b], preferred_element_type=F32)
-        gwo[...] = share if slots[b // 2] == OWN and b == 0 else gwo[...] + share
-    outs.append(pltpu.make_async_copy(gwo, gwo_hbm, o_sem.at[2 * chunks]))
+        share = jnp.dot(ot[:, now], held[now, :], preferred_element_type=F32)
+        gwo[...] = share if begins and low == 0 else gwo[...] + share
+    outs.append(pltpu.make_async_copy(gwo, gwo_hbm, o_sem.at[count]))
     outs[-1].start()
     for c in outs:
         c.wait()
@@ -519,9 +528,9 @@
             out_shape=[jax.ShapeDtypeStruct(*a) for a in (
                 ((tokens, hidden), BF16), ((ffn, tokens), BF16), ((ffn, tokens), BF16),
                 ((ffn, hidden), F32), ((ffn, hidden), F32), ((ffn, hidden), F32),
-                *[((half, hidden), BF16)] * 6)],
+                *[((half // 2, hidden), BF16)] * 4, *[((half, hidden), BF16)] * 4)],
             in_specs=[any_spec] * 8 + [pl.BlockSpec(memory_space=pltpu.VMEM), any_spec],
-            out_specs=[any_spec] * 12,
+            out_specs=[any_spec] * 14,
             scratch_shapes=[
                 pltpu.VMEM((ffn, hidden), BF16), pltpu.VMEM((ffn, hidden), BF16), pltpu.VMEM((ffn, hidden), BF16),
                 pltpu.VMEM((12, rows, hidden), BF16),
@@ -556,46 +565,60 @@
             compiler_params=pltpu.CompilerParams(vmem_limit_bytes=67_000_000),
         )(*arrays)
 
-    def attn(slots, halves, attn_t, w_out, *sofar):
-        (half, hidden), (width, tokens) = halves[0].shape, attn_t.shape
-        blocks = 2 * len(slots)
+    def attn(pieces, rows, attn_t, w_out, *sofar):
+        arrays, kinds = [p[0] for p in pieces], tuple(p[1:] for p in pieces)
+        hidden, (width, tokens) = arrays[0].shape[1], attn_t.shape
+        total, count = sum(a.shape[0] for a in arrays), len(arrays)
         dma = pltpu.SemaphoreType.DMA
         results = [jax.ShapeDtypeStruct((width, tokens), BF16), jax.ShapeDtypeStruct((width, hidden), F32)]
         if not sofar:
-            results.insert(0, jax.ShapeDtypeStruct((2 * half, hidden), BF16))
+            results.insert(0, jax.ShapeDtypeStruct((rows, hidden), BF16))
         return pl.pallas_call(
-            functools.partial(attn_kernel, n, slots),
-            in_specs=[any_space] * (2 * blocks + 2 + len(sofar)), out_specs=[any_space] * len(results),
+            functools.partial(attn_kernel, n, kinds, rows),
+            in_specs=[any_space] * (count + 2 + len(sofar)), out_specs=[any_space] * len(results),
             scratch_shapes=[
-                pltpu.VMEM((blocks, 2 * half, hidden), BF16), pltpu.VMEM((blocks, width, 2 * half), BF16),
-                pltpu.VMEM((width, hidden), BF16), pltpu.VMEM((blocks, width, 2 * half), BF16),
-                pltpu.VMEM((width, hidden), F32), dma((2 * blocks,)), dma((2 + blocks,)), dma((2 + blocks,))],
+                pltpu.VMEM((total, hidden), BF16), pltpu.VMEM((width, total), BF16), pltpu.VMEM((width, hidden), BF16),
+                pltpu.VMEM((width, total), BF16), pltpu.VMEM((width, hidden), F32),
+                dma((count,)), dma((2 + count,)), dma((2 + count,))],
             out_shape=results,
-            input_output_aliases={2 * blocks + 3: 0} if sofar else {},
-            cost_estimate=pl.CostEstimate(flops=600 * blocks * half * hidden, bytes_accessed=8 * blocks * half * hidden,
+            input_output_aliases={count + 3: 0} if sofar else {},
+            cost_estimate=pl.CostEstimate(flops=1200 * total * hidden, bytes_accessed=8 * total * hidden,
                                           transcendentals=0),
             compiler_params=pltpu.CompilerParams(vmem_limit_bytes=67_000_000),
-        )(*halves, attn_t, w_out, *sofar)
+        )(*arrays, attn_t, w_out, *sofar)
 
     def local_backward(x_norm, grad_y, u_gate, u_up, w_gate, w_up, w_down, x_in, gamma, grad_res, attn_out, w_out):
         attn_t = attn_out.T
-        _, _, _, gate_t, up_t, down, top, low, other_top, other_low, left_top, right_low = run_main(
+        rows = x_norm.shape[0]
+        half, part = rows // 2, rows // 4
+        (_, _, _, gate_t, up_t, down, top_a, top_b, low_a, low_b, other_top, other_low, left_top,
+         right_low) = run_main(
             x_norm, grad_y, u_gate.T, u_up.T, w_gate.T, w_up.T, w_down, x_in, gamma, grad_res)
 
-        left_low = go_right(low)
-        right_top = go_left(top)
+        def both(a, other, slot, row):
+            return [(a, slot, 0, row), (other, slot, 1, row)]
+
+        far_top, far_low = go_right(left_top), go_left(right_low)
+        left_low_a, right_top_a = go_right(low_a), go_left(top_a)
+        left_low_b, right_top_b = go_right(low_b), go_left(top_b)
         left_top_other, right_low_other = swap(left_top), swap(right_low)
         gate_t, up_t = settle(gate_t, up_t)
-        far_top = go_right(left_top)
-        far_low = go_left(right_low)
-        grad_sum, do_t, gwo = attn((OWN,), (top, low, other_top, other_low), attn_t, w_out)
-        left_low_other, right_top_other = swap(left_low), swap(right_top)
+        grad_sum, do_t, gwo = attn([
+            (top_a, OWN, 0, 0), (top_b, OWN, 0, part), (low_a, OWN, 0, half), (low_b, OWN, 0, half + part),
+            (other_top, OWN, 1, 0), (other_low, OWN, 1, half),
+            *both(left_top, left_top_other, LEFT, 0), *both(right_low, right_low_other, RIGHT, half)],
+            rows, attn_t, w_out)
         gw_down, = settle(down)
-        do_t, gwo = attn((RIGHT, LEFT), (
-            right_top, right_low, right_top_other, right_low_other,
-            left_top, left_low, left_top_other, left_low_other), attn_t, w_out, gwo, do_t)
-        far = (far_top, far_low, swap(far_top), swap(far_low))
-        do_t, gwo = attn((FAR,), far, attn_t, w_out, gwo, do_t)
+        far_top_other, far_low_other = swap(far_top), swap(far_low)
+        left_low_a_other, right_top_a_other = swap(left_low_a), swap(right_top_a)
+        do_t, gwo = attn([
+            *both(far_top, far_top_other, FAR, 0), *both(far_low, far_low_other, FAR, half),
+            *both(left_low_a, left_low_a_other, LEFT, half), *both(right_top_a, right_top_a_other, RIGHT, 0)],
+            rows, attn_t, w_out, gwo, do_t)
+        left_low_b_other, right_top_b_other = swap(left_low_b), swap(right_top_b)
+        do_t, gwo = attn([
+            *both(left_low_b, left_low_b_other, LEFT, half + part),
+            *both(right_top_b, right_top_b_other, RIGHT, part)], rows, attn_t, w_out, gwo, do_t)
         return grad_sum, do_t.T, gate_t.T, up_t.T, gw_down, gwo
 
     return jax.shard_map(

time: 250 us -> 251 us (level)
    ppermute x2 -> x3, waiting for transfers between devices: 15.1 us -> 31.4 us  [go_left(): return lax.ppermute(a, 'tp', left_of)]
    ppermute x2 -> x3, waiting for transfers between devices: 15 us -> 0.84 us  [go_right(): return lax.ppermute(a, 'tp', right_of)]
  transfers between devices with their start and end apart: 10 -> 14, of which waited for: 3 -> 3; matrix products, arithmetic and copies ran while one was open for 0% -> 0% of each run, Pallas kernels for 11% -> 11%
where the time goes in v2:
time: 251 us
  Pallas kernels  209 us (83%)
  waiting for transfers between devices  32.2 us (13%)
  starting transfers between devices  8.6 us (3%)
    pallas_call x1, Pallas kernels, run_main(): pl.pallas_call(functools.partial(main_kernel, n), out_shape=[jax.ShapeDty...  177 us
    ppermute x3, waiting for transfers between devices, go_left(): return lax.ppermute(a, 'tp', left_of)  31.4 us
    pallas_call x3, Pallas kernels, attn(): pl.pallas_call(functools.partial(attn_kernel, n, kinds, rows), in_specs=[...  16.2 us
    pallas_call x2, Pallas kernels, settle(): pl.pallas_call(settle_kernel, in_specs=[any_space] * len(arrays), out_spe...  15.7 us
  transfers between devices with their start and end apart: 14, of which 3 were waited for; matrix products, arithmetic and copies ran while one was open for 0% of the time, Pallas kernels for 11%

profile of v2, /device:TPU:113, one launch (start us, length us, event | category | flops | bytes accessed | tf_op | source)
XLA Modules:
  0.0 250.8 jit_solution(3332782346381831496)
XLA Ops:
  0.6 177.1 %shard_map.163 = (bf16[4096,1536]{1,0:T(8,128)(2,1)}, bf16[1120,4096]{1,0:T(8,128)(2,1)}, bf16[1120,4096]{1,0:T(8,128)(2,1)}, f32[1120,1536]{1,0:T(8,128)}, f32[...) custom-call(bf16[512,1536]{1,0:T(8,128)(2,1)} %x_hbm.1, ...), custom_call_target="tpu_custom_call" | custom-call | tf_op jit(solution)/shard_map/pallas_call | solution.py:526
  177.8 1.2 collective-permute-start.12
  179.0 0.3 collective-permute-start.6
  179.3 2.3 collective-permute-start.8
  181.6 0.0 collective-permute-start.4
  181.7 1.4 collective-permute-start.10
  183.1 6.1 %collective-permute-done.12.refs_6_ = bf16[128,1536]{1,0:T(8,128)(2,1)} collective-permute-done((bf16[128,1536]{1,0:T(8,128)(2,1)}, bf16[128,1536]{1,0:T(8,128)(2,1)}, u32[]{:S(2)}, u32[]{:S(2)}) %collective-permute-start.12) | collective-permute-done | bytes 393248 | tf_op jit(solution)/shard_map/ppermute | solution.py:510
  189.2 0.0 collective-permute-start.2
  189.2 25.3 %collective-permute-done.4.refs_2_ = bf16[128,1536]{1,0:T(8,128)(2,1)} collective-permute-done((bf16[128,1536]{1,0:T(8,128)(2,1)}, bf16[128,1536]{1,0:T(8,128)(2,1)}, u32[]{:S(2)}, u32[]{:S(2)}) %collective-permute-start.4) | collective-permute-done | bytes 393248 | tf_op jit(solution)/shard_map/ppermute | solution.py:510
  214.5 0.5 collective-permute-start
  215.0 0.0 collective-permute-done.10.refs_4_
  215.0 0.0 collective-permute-start.1
  215.0 0.8 collective-permute-done.2.refs_0_
  215.8 1.5 collective-permute-start.13
  217.3 0.0 collective-permute-done.6.refs_0_
  217.3 0.0 collective-permute-start.7
  217.3 0.0 collective-permute-done.8.refs_2_
  217.3 0.5 collective-permute-start.9
  217.8 10.0 %shard_map.167 = (f32[1120,1536]{1,0:T(8,128)}, f32[1120,1536]{1,0:T(8,128)}) custom-call(f32[1120,1536]{1,0:T(8,128)} %get-tuple-element.40.refs_0_, f32[1120,1536]{1,0:T(8,128)} %get-tuple-element.41.refs_1_), custom_call_target="tpu_custom_call" | custom-call | flops 6881280000 | bytes 27525120 | tf_op jit(solution)/shard_map/pallas_call | solution.py:557
  227.9 0.0 collective-permute-done.13.refs_7_
  227.9 0.1 collective-permute-start.11
  228.0 5.7 %shard_map.168 = f32[1120,1536]{1,0:T(8,128)} custom-call(f32[1120,1536]{1,0:T(8,128)} %get-tuple-element.44.refs_0_), custom_call_target="tpu_custom_call" | custom-call | flops 3440640000 | bytes 13762560 | tf_op jit(solution)/shard_map/pallas_call | solution.py:557
  233.7 0.0 collective-permute-done.refs_7_
  233.8 0.5 collective-permute-start.5
  234.3 0.0 collective-permute-done.1.refs_9_
  234.3 0.1 collective-permute-start.3
  234.4 6.5 %shard_map.164 = (bf16[512,1536]{1,0:T(8,128)(2,1)}, bf16[192,4096]{1,0:T(8,128)(2,1)}, f32[192,1536]{1,0:T(8,128)}) custom-call(bf16[128,1536]{1,0:T(8,128)(2,1)} %get-tuple-element.26.refs_0_, bf16[128,1536]{1,0:T(8,128)(2,1)} %get-tuple-element.27.refs_1_, bf16[128,1536]{1,0:T(8,128)(2,1)} %get-tuple-element.28.refs_2_, ...), custom_call_target="tpu_custom_call" | custom-call | flops 3774873600 | bytes 25165824 | tf_op jit(solution)/shard_map/pallas_call | solution.py:576
  240.8 0.0 collective-permute-done.11.refs_5_
  240.9 0.0 collective-permute-done.7.refs_1_
  240.9 0.0 collective-permute-done.9.refs_3_
  240.9 5.8 %shard_map.165 = (bf16[192,4096]{1,0:T(8,128)(2,1)}, f32[192,1536]{1,0:T(8,128)}) custom-call(bf16[256,1536]{1,0:T(8,128)(2,1)} %collective-permute-done.6.refs_0_, bf16[256,1536]{1,0:T(8,128)(2,1)} %collective-permute-done.7.refs_1_, bf16[256,1536]{1,0:T(8,128)(2,1)} %collective-permute-done.8.refs_2_, ...), custom_call_target="tpu_custom_call", output_to_operand_aliasing={{0}: (11, {})} | custom-call | flops 2831155200 | bytes 18874368 | tf_op jit(solution)/shard_map/pallas_call | solution.py:576
  246.7 0.0 collective-permute-done.5.refs_3_
  246.7 0.0 collective-permute-done.3.refs_1_
  246.7 3.9 %shard_map.166 = (bf16[192,4096]{1,0:T(8,128)(2,1)}, f32[192,1536]{1,0:T(8,128)}) custom-call(bf16[128,1536]{1,0:T(8,128)(2,1)} %collective-permute-done.2.refs_0_, bf16[128,1536]{1,0:T(8,128)(2,1)} %collective-permute-done.3.refs_1_, bf16[128,1536]{1,0:T(8,128)(2,1)} %collective-permute-done.4.refs_2_, ...), custom_call_target="tpu_custom_call", output_to_operand_aliasing={{0}: (7, {})} | custom-call | flops 943718400 | bytes 6291456 | tf_op jit(solution)/shard_map/pallas_call | solution.py:576
Async XLA Ops:
  177.8 11.4 %collective-permute-start.12 = (bf16[128,1536]{1,0:T(8,128)(2,1)}, bf16[128,1536]{1,0:T(8,128)(2,1)}, u32[]{:S(2)}, u32[]{:S(2)}) collective-permute-start(bf16[128,1536]{1,0:T(8,128)(2,1)} %get-tuple-element.26.refs_0_), channel_id=1, source_target_pairs={{0,6},{1,7},{2,0},{3,1},{4,2},{5,3},{6,4},{7,5},{8,14},{9,15},{10,... | collective-permute-start | bytes 1179656 | tf_op jit(solution)/shard_map/ppermute | solution.py:510
  179.0 38.3 %collective-permute-start.6 = (bf16[256,1536]{1,0:T(8,128)(2,1)}, bf16[256,1536]{1,0:T(8,128)(2,1)}, u32[]{:S(2)}, u32[]{:S(2)}) collective-permute-start(bf16[256,1536]{1,0:T(8,128)(2,1)} %get-tuple-element.32.refs_6_), channel_id=1, source_target_pairs={{0,2},{1,3},{2,4},{3,5},{4,6},{5,7},{6,0},{7,1},{8,10},{9,11},{10,... | collective-permute-start | bytes 2359304 | tf_op jit(solution)/shard_map/ppermute | solution.py:507
  179.3 38.0 %collective-permute-start.8 = (bf16[256,1536]{1,0:T(8,128)(2,1)}, bf16[256,1536]{1,0:T(8,128)(2,1)}, u32[]{:S(2)}, u32[]{:S(2)}) collective-permute-start(bf16[256,1536]{1,0:T(8,128)(2,1)} %get-tuple-element.33.refs_8_), channel_id=1, source_target_pairs={{0,6},{1,7},{2,0},{3,1},{4,2},{5,3},{6,4},{7,5},{8,14},{9,15},{10,... | collective-permute-start | bytes 2359304 | tf_op jit(solution)/shard_map/ppermute | solution.py:510
  181.6 32.8 %collective-permute-start.4 = (bf16[128,1536]{1,0:T(8,128)(2,1)}, bf16[128,1536]{1,0:T(8,128)(2,1)}, u32[]{:S(2)}, u32[]{:S(2)}) collective-permute-start(bf16[128,1536]{1,0:T(8,128)(2,1)} %get-tuple-element.27.refs_1_), channel_id=1, source_target_pairs={{0,6},{1,7},{2,0},{3,1},{4,2},{5,3},{6,4},{7,5},{8,14},{9,15},{10,... | collective-permute-start | bytes 1179656 | tf_op jit(solution)/shard_map/ppermute | solution.py:510
  181.7 33.3 %collective-permute-start.10 = (bf16[128,1536]{1,0:T(8,128)(2,1)}, bf16[128,1536]{1,0:T(8,128)(2,1)}, u32[]{:S(2)}, u32[]{:S(2)}) collective-permute-start(bf16[128,1536]{1,0:T(8,128)(2,1)} %get-tuple-element.28.refs_2_), channel_id=1, source_target_pairs={{0,2},{1,3},{2,4},{3,5},{4,6},{5,7},{6,0},{7,1},{8,10},{9,11},{10,... | collective-permute-start | bytes 1179656 | tf_op jit(solution)/shard_map/ppermute | solution.py:507
  189.2 26.6 %collective-permute-start.2 = (bf16[128,1536]{1,0:T(8,128)(2,1)}, bf16[128,1536]{1,0:T(8,128)(2,1)}, u32[]{:S(2)}, u32[]{:S(2)}) collective-permute-start(bf16[128,1536]{1,0:T(8,128)(2,1)} %get-tuple-element.29.refs_3_), channel_id=1, source_target_pairs={{0,2},{1,3},{2,4},{3,5},{4,6},{5,7},{6,0},{7,1},{8,10},{9,11},{10,... | collective-permute-start | bytes 1179656 | tf_op jit(solution)/shard_map/ppermute | solution.py:507
  214.5 19.3 %collective-permute-start = (bf16[256,1536]{1,0:T(8,128)(2,1)}, bf16[256,1536]{1,0:T(8,128)(2,1)}, u32[]{:S(2)}, u32[]{:S(2)}) collective-permute-start(bf16[256,1536]{1,0:T(8,128)(2,1)} %get-tuple-element.32.refs_6_), channel_id=1, source_target_pairs={{0,1},{1,0},{2,3},{3,2},{4,5},{5,4},{6,7},{7,6},{8,9},{9,8},{10,11... | collective-permute-start | bytes 2359304 | tf_op jit(solution)/shard_map/ppermute | solution.py:513
  215.0 19.3 %collective-permute-start.1 = (bf16[256,1536]{1,0:T(8,128)(2,1)}, bf16[256,1536]{1,0:T(8,128)(2,1)}, u32[]{:S(2)}, u32[]{:S(2)}) collective-permute-start(bf16[256,1536]{1,0:T(8,128)(2,1)} %get-tuple-element.33.refs_8_), channel_id=1, source_target_pairs={{0,1},{1,0},{2,3},{3,2},{4,5},{5,4},{6,7},{7,6},{8,9},{9,8},{10,11... | collective-permute-start | bytes 2359304 | tf_op jit(solution)/shard_map/ppermute | solution.py:513
  215.8 12.0 %collective-permute-start.13 = (bf16[128,1536]{1,0:T(8,128)(2,1)}, bf16[128,1536]{1,0:T(8,128)(2,1)}, u32[]{:S(2)}, u32[]{:S(2)}) collective-permute-start(bf16[128,1536]{1,0:T(8,128)(2,1)} %collective-permute-done.12.refs_6_), channel_id=1, source_target_pairs={{0,1},{1,0},{2,3},{3,2},{4,5},{5,4},{6,7},{7,6},{8,9},{9,8},{10,11... | collective-permute-start | bytes 1179656 | tf_op jit(solution)/shard_map/ppermute | solution.py:513
  217.3 23.6 %collective-permute-start.7 = (bf16[256,1536]{1,0:T(8,128)(2,1)}, bf16[256,1536]{1,0:T(8,128)(2,1)}, u32[]{:S(2)}, u32[]{:S(2)}) collective-permute-start(bf16[256,1536]{1,0:T(8,128)(2,1)} %collective-permute-done.6.refs_0_), channel_id=1, source_target_pairs={{0,1},{1,0},{2,3},{3,2},{4,5},{5,4},{6,7},{7,6},{8,9},{9,8},{10,11... | collective-permute-start | bytes 2359304 | tf_op jit(solution)/shard_map/ppermute | solution.py:513
  217.3 23.6 %collective-permute-start.9 = (bf16[256,1536]{1,0:T(8,128)(2,1)}, bf16[256,1536]{1,0:T(8,128)(2,1)}, u32[]{:S(2)}, u32[]{:S(2)}) collective-permute-start(bf16[256,1536]{1,0:T(8,128)(2,1)} %collective-permute-done.8.refs_2_), channel_id=1, source_target_pairs={{0,1},{1,0},{2,3},{3,2},{4,5},{5,4},{6,7},{7,6},{8,9},{9,8},{10,11... | collective-permute-start | bytes 2359304 | tf_op jit(solution)/shard_map/ppermute | solution.py:513
  227.9 13.0 %collective-permute-start.11 = (bf16[128,1536]{1,0:T(8,128)(2,1)}, bf16[128,1536]{1,0:T(8,128)(2,1)}, u32[]{:S(2)}, u32[]{:S(2)}) collective-permute-start(bf16[128,1536]{1,0:T(8,128)(2,1)} %collective-permute-done.10.refs_4_), channel_id=1, source_target_pairs={{0,1},{1,0},{2,3},{3,2},{4,5},{5,4},{6,7},{7,6},{8,9},{9,8},{10,11... | collective-permute-start | bytes 1179656 | tf_op jit(solution)/shard_map/ppermute | solution.py:513
  233.8 12.9 %collective-permute-start.5 = (bf16[128,1536]{1,0:T(8,128)(2,1)}, bf16[128,1536]{1,0:T(8,128)(2,1)}, u32[]{:S(2)}, u32[]{:S(2)}) collective-permute-start(bf16[128,1536]{1,0:T(8,128)(2,1)} %collective-permute-done.4.refs_2_), channel_id=1, source_target_pairs={{0,1},{1,0},{2,3},{3,2},{4,5},{5,4},{6,7},{7,6},{8,9},{9,8},{10,11... | collective-permute-start | bytes 1179656 | tf_op jit(solution)/shard_map/ppermute | solution.py:513
  234.3 12.4 %collective-permute-start.3 = (bf16[128,1536]{1,0:T(8,128)(2,1)}, bf16[128,1536]{1,0:T(8,128)(2,1)}, u32[]{:S(2)}, u32[]{:S(2)}) collective-permute-start(bf16[128,1536]{1,0:T(8,128)(2,1)} %collective-permute-done.2.refs_0_), channel_id=1, source_target_pairs={{0,1},{1,0},{2,3},{3,2},{4,5},{5,4},{6,7},{7,6},{8,9},{9,8},{10,11... | collective-permute-start | bytes 1179656 | tf_op jit(solution)/shard_map/ppermute | solution.py:513

commit v3 on v2

--- a/solution.py
+++ b/solution.py
@@ -553,7 +553,7 @@
 
     def settle(*arrays):
         lines, hidden = arrays[0].shape
-        slots = min(16, 10 * len(arrays))
+        slots = 10 * len(arrays)
         return pl.pallas_call(
             settle_kernel,
             in_specs=[any_space] * len(arrays), out_specs=[any_space] * len(arrays),
@@ -602,13 +602,12 @@
         left_low_a, right_top_a = go_right(low_a), go_left(top_a)
         left_low_b, right_top_b = go_right(low_b), go_left(top_b)
         left_top_other, right_low_other = swap(left_top), swap(right_low)
-        gate_t, up_t = settle(gate_t, up_t)
+        gate_t, up_t, gw_down = settle(gate_t, up_t, down)
         grad_sum, do_t, gwo = attn([
             (top_a, OWN, 0, 0), (top_b, OWN, 0, part), (low_a, OWN, 0, half), (low_b, OWN, 0, half + part),
             (other_top, OWN, 1, 0), (other_low, OWN, 1, half),
             *both(left_top, left_top_other, LEFT, 0), *both(right_low, right_low_other, RIGHT, half)],
             rows, attn_t, w_out)
-        gw_down, = settle(down)
         far_top_other, far_low_other = swap(far_top), swap(far_low)
         left_low_a_other, right_top_a_other = swap(left_low_a), swap(right_top_a)
         do_t, gwo = attn([

time: 251 us -> 251 us (level)
    ppermute x3, waiting for transfers between devices: 31.4 us -> 15.6 us  [go_left(): return lax.ppermute(a, 'tp', left_of)]
    ppermute x3, waiting for transfers between devices: 0.84 us -> 16.2 us  [go_right(): return lax.ppermute(a, 'tp', right_of)]
    pallas_call x2 -> x1, Pallas kernels: 15.7 us -> 14.3 us  [settle(): pl.pallas_call(settle_kernel, in_specs=[any_space] * len(arrays), out_spe...]
  transfers between devices with their start and end apart: 14 -> 14, of which waited for: 3 -> 4; matrix products, arithmetic and copies ran while one was open for 0% -> 0% of each run, Pallas kernels for 11% -> 11%
where the time goes in v3:
time: 251 us; the launch traced here: 250 us
  Pallas kernels  208 us (83%)
  waiting for transfers between devices  31.8 us (13%)
  starting transfers between devices  9.31 us (4%)
    pallas_call x1, Pallas kernels, run_main(): pl.pallas_call(functools.partial(main_kernel, n), out_shape=[jax.ShapeDty...  177 us
    pallas_call x3, Pallas kernels, attn(): pl.pallas_call(functools.partial(attn_kernel, n, kinds, rows), in_specs=[...  16.2 us
    ppermute x3, waiting for transfers between devices, go_right(): return lax.ppermute(a, 'tp', right_of)  16.2 us
    ppermute x3, waiting for transfers between devices, go_left(): return lax.ppermute(a, 'tp', left_of)  15.6 us
    pallas_call x1, Pallas kernels, settle(): pl.pallas_call(settle_kernel, in_specs=[any_space] * len(arrays), out_spe...  14.3 us
    ppermute x8, starting transfers between devices, swap(): return lax.ppermute(a, 'tp', partner_of)  5.07 us
  transfers between devices with their start and end apart: 14, of which 4 were waited for; matrix products, arithmetic and copies ran while one was open for 0% of the time, Pallas kernels for 11%

profile of v3, /device:TPU:113, one launch (start us, length us, event | category | flops | bytes accessed | tf_op | source)
XLA Modules:
  0.0 250.4 jit_solution(16141139622786847347)
XLA Ops:
  0.6 177.1 %shard_map.163 = (bf16[4096,1536]{1,0:T(8,128)(2,1)}, bf16[1120,4096]{1,0:T(8,128)(2,1)}, bf16[1120,4096]{1,0:T(8,128)(2,1)}, f32[1120,1536]{1,0:T(8,128)}, f32[...) custom-call(bf16[512,1536]{1,0:T(8,128)(2,1)} %x_hbm.1, ...), custom_call_target="tpu_custom_call" | custom-call | tf_op jit(solution)/shard_map/pallas_call | solution.py:526
  177.8 1.2 collective-permute-start.12
  179.0 0.4 collective-permute-start.4
  179.3 1.1 collective-permute-start.6
  180.4 1.6 collective-permute-start.8
  182.0 0.0 collective-permute-start.10
  182.0 7.2 %collective-permute-done.12.refs_6_ = bf16[128,1536]{1,0:T(8,128)(2,1)S(1)} collective-permute-done((bf16[128,1536]{1,0:T(8,128)(2,1)}, bf16[128,1536]{1,0:T(8,128)(2,1)S(1)}, u32[]{:S(2)}, u32[]{:S(2)}) %collective-permute-start.12) | collective-permute-done | bytes 393248 | tf_op jit(solution)/shard_map/ppermute | solution.py:510
  189.2 0.0 copy-start
  189.2 0.0 collective-permute-start.2
  189.2 8.4 %collective-permute-done.4.refs_2_ = bf16[128,1536]{1,0:T(8,128)(2,1)} collective-permute-done((bf16[128,1536]{1,0:T(8,128)(2,1)}, bf16[128,1536]{1,0:T(8,128)(2,1)}, u32[]{:S(2)}, u32[]{:S(2)}) %collective-permute-start.4) | collective-permute-done | bytes 393248 | tf_op jit(solution)/shard_map/ppermute | solution.py:510
  197.6 0.0 copy-done
  197.6 0.6 collective-permute-start.13
  198.2 9.8 %collective-permute-done.10.refs_4_ = bf16[128,1536]{1,0:T(8,128)(2,1)} collective-permute-done((bf16[128,1536]{1,0:T(8,128)(2,1)}, bf16[128,1536]{1,0:T(8,128)(2,1)}, u32[]{:S(2)}, u32[]{:S(2)}) %collective-permute-start.10) | collective-permute-done | bytes 393248 | tf_op jit(solution)/shard_map/ppermute | solution.py:507
  208.0 2.0 collective-permute-start
  210.1 6.4 %collective-permute-done.2.refs_0_ = bf16[128,1536]{1,0:T(8,128)(2,1)} collective-permute-done((bf16[128,1536]{1,0:T(8,128)(2,1)}, bf16[128,1536]{1,0:T(8,128)(2,1)}, u32[]{:S(2)}, u32[]{:S(2)}) %collective-permute-start.2) | collective-permute-done | bytes 393248 | tf_op jit(solution)/shard_map/ppermute | solution.py:507
  216.4 1.2 collective-permute-start.1
  217.7 0.0 collective-permute-done.13.refs_7_
  217.7 0.0 copy-start.1
  217.7 0.7 copy-done.1
  218.4 0.0 collective-permute-start.11
  218.4 0.0 collective-permute-done.6.refs_0_
  218.4 0.5 collective-permute-start.7
  218.9 0.0 collective-permute-done.8.refs_2_
  218.9 0.1 collective-permute-start.9
  219.0 14.3 %shard_map.167 = (f32[1120,1536]{1,0:T(8,128)}, f32[1120,1536]{1,0:T(8,128)}, f32[1120,1536]{1,0:T(8,128)}) custom-call(f32[1120,1536]{1,0:T(8,128)} %get-tuple-element.41.refs_0_, f32[1120,1536]{1,0:T(8,128)} %get-tuple-element.42.refs_1_, f32[1120,1536]{1,0:T(8,128)} %get-tuple-element.43.refs_2_), custom_call_target="tpu_custom_call" | custom-call | flops 10321920000 | bytes 41287680 | tf_op jit(solution)/shard_map/pallas_call | solution.py:557
  233.4 0.0 collective-permute-done.refs_7_
  233.4 0.5 collective-permute-start.5
  233.9 0.0 collective-permute-done.1.refs_9_
  233.9 0.1 collective-permute-start.3
  234.0 6.5 %shard_map.164 = (bf16[512,1536]{1,0:T(8,128)(2,1)}, bf16[192,4096]{1,0:T(8,128)(2,1)}, f32[192,1536]{1,0:T(8,128)}) custom-call(bf16[128,1536]{1,0:T(8,128)(2,1)} %get-tuple-element.27.refs_0_, bf16[128,1536]{1,0:T(8,128)(2,1)} %get-tuple-element.28.refs_1_, bf16[128,1536]{1,0:T(8,128)(2,1)} %get-tuple-element.29.refs_2_, ...), custom_call_target="tpu_custom_call" | custom-call | flops 3774873600 | bytes 25165824 | tf_op jit(solution)/shard_map/pallas_call | solution.py:576
  240.5 0.0 collective-permute-done.11.refs_5_
  240.5 0.0 collective-permute-done.7.refs_1_
  240.5 0.0 collective-permute-done.9.refs_3_
  240.5 5.8 %shard_map.165 = (bf16[192,4096]{1,0:T(8,128)(2,1)}, f32[192,1536]{1,0:T(8,128)}) custom-call(bf16[256,1536]{1,0:T(8,128)(2,1)} %collective-permute-done.6.refs_0_, bf16[256,1536]{1,0:T(8,128)(2,1)} %collective-permute-done.7.refs_1_, bf16[256,1536]{1,0:T(8,128)(2,1)} %collective-permute-done.8.refs_2_, ...), custom_call_target="tpu_custom_call", output_to_operand_aliasing={{0}: (11, {})} | custom-call | flops 2831155200 | bytes 18874368 | tf_op jit(solution)/shard_map/pallas_call | solution.py:576
  246.3 0.0 collective-permute-done.5.refs_3_
  246.3 0.0 collective-permute-done.3.refs_1_
  246.3 3.9 %shard_map.166 = (bf16[192,4096]{1,0:T(8,128)(2,1)}, f32[192,1536]{1,0:T(8,128)}) custom-call(bf16[128,1536]{1,0:T(8,128)(2,1)} %collective-permute-done.2.refs_0_, bf16[128,1536]{1,0:T(8,128)(2,1)} %collective-permute-done.3.refs_1_, bf16[128,1536]{1,0:T(8,128)(2,1)} %collective-permute-done.4.refs_2_, ...), custom_call_target="tpu_custom_call", output_to_operand_aliasing={{0}: (7, {})} | custom-call | flops 943718400 | bytes 6291456 | tf_op jit(solution)/shard_map/pallas_call | solution.py:576
Async XLA Ops:
  177.8 11.4 %collective-permute-start.12 = (bf16[128,1536]{1,0:T(8,128)(2,1)}, bf16[128,1536]{1,0:T(8,128)(2,1)S(1)}, u32[]{:S(2)}, u32[]{:S(2)}) collective-permute-start(bf16[128,1536]{1,0:T(8,128)(2,1)} %get-tuple-element.27.refs_0_), channel_id=1, source_target_pairs={{0,6},{1,7},{2,0},{3,1},{4,2},{5,3},{6,4},{7,5},{8,14},{9,15},{10,... | collective-permute-start | bytes 1179656 | tf_op jit(solution)/shard_map/ppermute | solution.py:510
  179.0 18.6 %collective-permute-start.4 = (bf16[128,1536]{1,0:T(8,128)(2,1)}, bf16[128,1536]{1,0:T(8,128)(2,1)}, u32[]{:S(2)}, u32[]{:S(2)}) collective-permute-start(bf16[128,1536]{1,0:T(8,128)(2,1)} %get-tuple-element.28.refs_1_), channel_id=1, source_target_pairs={{0,6},{1,7},{2,0},{3,1},{4,2},{5,3},{6,4},{7,5},{8,14},{9,15},{10,... | collective-permute-start | bytes 1179656 | tf_op jit(solution)/shard_map/ppermute | solution.py:510
  179.3 39.1 %collective-permute-start.6 = (bf16[256,1536]{1,0:T(8,128)(2,1)}, bf16[256,1536]{1,0:T(8,128)(2,1)}, u32[]{:S(2)}, u32[]{:S(2)}) collective-permute-start(bf16[256,1536]{1,0:T(8,128)(2,1)} %get-tuple-element.33.refs_6_), channel_id=1, source_target_pairs={{0,2},{1,3},{2,4},{3,5},{4,6},{5,7},{6,0},{7,1},{8,10},{9,11},{10,... | collective-permute-start | bytes 2359304 | tf_op jit(solution)/shard_map/ppermute | solution.py:507
  180.4 38.5 %collective-permute-start.8 = (bf16[256,1536]{1,0:T(8,128)(2,1)}, bf16[256,1536]{1,0:T(8,128)(2,1)}, u32[]{:S(2)}, u32[]{:S(2)}) collective-permute-start(bf16[256,1536]{1,0:T(8,128)(2,1)} %get-tuple-element.34.refs_8_), channel_id=1, source_target_pairs={{0,6},{1,7},{2,0},{3,1},{4,2},{5,3},{6,4},{7,5},{8,14},{9,15},{10,... | collective-permute-start | bytes 2359304 | tf_op jit(solution)/shard_map/ppermute | solution.py:510
  182.0 26.0 %collective-permute-start.10 = (bf16[128,1536]{1,0:T(8,128)(2,1)}, bf16[128,1536]{1,0:T(8,128)(2,1)}, u32[]{:S(2)}, u32[]{:S(2)}) collective-permute-start(bf16[128,1536]{1,0:T(8,128)(2,1)} %get-tuple-element.29.refs_2_), channel_id=1, source_target_pairs={{0,2},{1,3},{2,4},{3,5},{4,6},{5,7},{6,0},{7,1},{8,10},{9,11},{10,... | collective-permute-start | bytes 1179656 | tf_op jit(solution)/shard_map/ppermute | solution.py:507
  189.2 8.4 %copy-start = (bf16[128,1536]{1,0:T(8,128)(2,1)}, bf16[128,1536]{1,0:T(8,128)(2,1)S(1)}, u32[]{:S(2)}) copy-start(bf16[128,1536]{1,0:T(8,128)(2,1)S(1)} %collective-permute-done.12.refs_6_) | copy-start | bytes 1179652
  189.2 27.2 %collective-permute-start.2 = (bf16[128,1536]{1,0:T(8,128)(2,1)}, bf16[128,1536]{1,0:T(8,128)(2,1)}, u32[]{:S(2)}, u32[]{:S(2)}) collective-permute-start(bf16[128,1536]{1,0:T(8,128)(2,1)} %get-tuple-element.30.refs_3_), channel_id=1, source_target_pairs={{0,2},{1,3},{2,4},{3,5},{4,6},{5,7},{6,0},{7,1},{8,10},{9,11},{10,... | collective-permute-start | bytes 1179656 | tf_op jit(solution)/shard_map/ppermute | solution.py:507
  197.6 20.0 %collective-permute-start.13 = (bf16[128,1536]{1,0:T(8,128)(2,1)S(1)}, bf16[128,1536]{1,0:T(8,128)(2,1)S(1)}, u32[]{:S(2)}, u32[]{:S(2)}) collective-permute-start(bf16[128,1536]{1,0:T(8,128)(2,1)S(1)} %collective-permute-done.12.refs_6_), channel_id=1, source_target_pairs={{0,1},{1,0},{2,3},{3,2},{4,5},{5,4},{6,7},{7,6},{8,9},{9,8},{10,11... | collective-permute-start | bytes 1179656 | tf_op jit(solution)/shard_map/ppermute | solution.py:513
  208.0 25.3 %collective-permute-start = (bf16[256,1536]{1,0:T(8,128)(2,1)}, bf16[256,1536]{1,0:T(8,128)(2,1)}, u32[]{:S(2)}, u32[]{:S(2)}) collective-permute-start(bf16[256,1536]{1,0:T(8,128)(2,1)} %get-tuple-element.33.refs_6_), channel_id=1, source_target_pairs={{0,1},{1,0},{2,3},{3,2},{4,5},{5,4},{6,7},{7,6},{8,9},{9,8},{10,11... | collective-permute-start | bytes 2359304 | tf_op jit(solution)/shard_map/ppermute | solution.py:513
  216.4 17.4 %collective-permute-start.1 = (bf16[256,1536]{1,0:T(8,128)(2,1)}, bf16[256,1536]{1,0:T(8,128)(2,1)}, u32[]{:S(2)}, u32[]{:S(2)}) collective-permute-start(bf16[256,1536]{1,0:T(8,128)(2,1)} %get-tuple-element.34.refs_8_), channel_id=1, source_target_pairs={{0,1},{1,0},{2,3},{3,2},{4,5},{5,4},{6,7},{7,6},{8,9},{9,8},{10,11... | collective-permute-start | bytes 2359304 | tf_op jit(solution)/shard_map/ppermute | solution.py:513
  217.7 0.7 copy-start.1
  218.4 22.1 %collective-permute-start.11 = (bf16[128,1536]{1,0:T(8,128)(2,1)}, bf16[128,1536]{1,0:T(8,128)(2,1)}, u32[]{:S(2)}, u32[]{:S(2)}) collective-permute-start(bf16[128,1536]{1,0:T(8,128)(2,1)} %collective-permute-done.10.refs_4_), channel_id=1, source_target_pairs={{0,1},{1,0},{2,3},{3,2},{4,5},{5,4},{6,7},{7,6},{8,9},{9,8},{10,11... | collective-permute-start | bytes 1179656 | tf_op jit(solution)/shard_map/ppermute | solution.py:513
  218.4 22.1 %collective-permute-start.7 = (bf16[256,1536]{1,0:T(8,128)(2,1)}, bf16[256,1536]{1,0:T(8,128)(2,1)}, u32[]{:S(2)}, u32[]{:S(2)}) collective-permute-start(bf16[256,1536]{1,0:T(8,128)(2,1)} %collective-permute-done.6.refs_0_), channel_id=1, source_target_pairs={{0,1},{1,0},{2,3},{3,2},{4,5},{5,4},{6,7},{7,6},{8,9},{9,8},{10,11... | collective-permute-start | bytes 2359304 | tf_op jit(solution)/shard_map/ppermute | solution.py:513
  218.9 21.6 %collective-permute-start.9 = (bf16[256,1536]{1,0:T(8,128)(2,1)}, bf16[256,1536]{1,0:T(8,128)(2,1)}, u32[]{:S(2)}, u32[]{:S(2)}) collective-permute-start(bf16[256,1536]{1,0:T(8,128)(2,1)} %collective-permute-done.8.refs_2_), channel_id=1, source_target_pairs={{0,1},{1,0},{2,3},{3,2},{4,5},{5,4},{6,7},{7,6},{8,9},{9,8},{10,11... | collective-permute-start | bytes 2359304 | tf_op jit(solution)/shard_map/ppermute | solution.py:513
  233.4 12.9 %collective-permute-start.5 = (bf16[128,1536]{1,0:T(8,128)(2,1)}, bf16[128,1536]{1,0:T(8,128)(2,1)}, u32[]{:S(2)}, u32[]{:S(2)}) collective-permute-start(bf16[128,1536]{1,0:T(8,128)(2,1)} %collective-permute-done.4.refs_2_), channel_id=1, source_target_pairs={{0,1},{1,0},{2,3},{3,2},{4,5},{5,4},{6,7},{7,6},{8,9},{9,8},{10,11... | collective-permute-start | bytes 1179656 | tf_op jit(solution)/shard_map/ppermute | solution.py:513
  233.9 12.4 %collective-permute-start.3 = (bf16[128,1536]{1,0:T(8,128)(2,1)}, bf16[128,1536]{1,0:T(8,128)(2,1)}, u32[]{:S(2)}, u32[]{:S(2)}) collective-permute-start(bf16[128,1536]{1,0:T(8,128)(2,1)} %collective-permute-done.2.refs_0_), channel_id=1, source_target_pairs={{0,1},{1,0},{2,3},{3,2},{4,5},{5,4},{6,7},{7,6},{8,9},{9,8},{10,11... | collective-permute-start | bytes 1179656 | tf_op jit(solution)/shard_map/ppermute | solution.py:513
